TPU v7x, 32 devices: a whole 2x2x4 slice. The times are simulated.
32 devices in a mesh: section: 2 (over y), ep: 16 (over z, x, core).
Axes of the slice: x: 2, y: 2, z: 4, core: 2. Of those that a mesh axis runs over, the one named last changes fastest.
Arguments:
- inputs: bfloat16 [2, 2048, 1536], P('section', 'ep'), may hold values from -6 to 6
- upstream: bfloat16 [2, 2048, 1536], P('section', 'ep'), may hold values from -6 to 6
- gate_saved: bfloat16 [2, 2048, 8, 384], P('section', 'ep'), may hold values from -6 to 6
- expert_ids: int32 [2, 2048, 8], P('section', 'ep'), may hold values from 0 to 31, all different within a row; in each aligned block of 128 rows (0 to 127, 128 to 255, ..., all dimensions but the last counted through in order) at most 48 rows name the same one
- route_weights: float32 [2, 2048, 8], P('section', 'ep'), may hold values from 0.05 to 0.5
- w_up: bfloat16 [2, 32, 1536, 384], P('section', 'ep'), may hold values from -0.15625 to 0.15625
- w_down: bfloat16 [2, 32, 384, 1536], P('section', 'ep'), may hold values from -0.3125 to 0.3125
Outputs:
- delivered: bfloat16 [2, 2048, 1536], P('section', 'ep')
- grad_up: bfloat16 [2, 32, 1536, 384], P('section', 'ep')
- grad_down: bfloat16 [2, 32, 384, 1536], P('section', 'ep')
Inputs may be any that keep to these rules, and one draw needn't show every extreme that they name: `expert_ids`: each row names 8 different experts. In the rows of one device no expert is named more than 48 times, and in every draw some expert is named exactly 48 times in the rows of some device; every expert is named somewhere.
All inputs are finite; a program needn't handle non-finite values.
Results may differ from a plain program's by a relative error of at most 0.012.
Values may be sent and summed in bfloat16 or wider, within the bound.
No kernel may reach another device: no remote copies, remote signals or barrier semaphores. Data moves between devices by JAX's collectives and lax.ppermute only.
A program may use at most 192 MiB of HBM per device.

v0:
```python
import functools

import jax
import jax.numpy as jnp
from jax import lax
from jax.experimental import pallas as pl
from jax.experimental.pallas import tpu as pltpu
from jax.sharding import PartitionSpec as P


F32 = jnp.float32
BF16 = jnp.bfloat16
EXTRA = 8
NT = (((1,), (1,)), ((), ()))
TN = (((0,), (0,)), ((), ()))


def dot(a, b, dims=(((1,), (0,)), ((), ()))):
    return lax.dot_general(a, b, dims, preferred_element_type=F32)


class Grid:
    def __init__(self):
        self.sections = lax.axis_size("section")
        self.size = lax.axis_size("ep")
        self.chips = self.size // 2
        bits = self.chips.bit_length() - 1
        self.z = 1 << ((bits + 1) // 2)
        self.x = self.chips // self.z

    def move(self, block, target, shift=0):
        pairs = []
        for s in range(self.sections):
            for i in range(self.size):
                to = target(i // 2 // self.x, i // 2 % self.x, i % 2)
                if to is not None:
                    z, x, core = to
                    there = (z * self.x + x) * 2 + core
                    pairs.append((s * self.size + i, (s + shift) % self.sections * self.size + there))
        return lax.ppermute(block, ("section", "ep"), pairs)


def prep_kernel(top, cap, local, ids_ref, act_ref, *out_refs):
    index = lax.axis_index("ep")
    chip, core = index // 2, index % 2
    rows = act_ref.shape[0]
    experts = len(out_refs) * 2 * local
    ids = ids_ref[...]
    named = lax.broadcasted_iota(jnp.int32, (experts, rows), 0) == ids
    upper = lax.broadcasted_iota(jnp.int32, (rows, rows), 0) <= lax.broadcasted_iota(jnp.int32, (rows, rows), 1)
    count = dot(named.astype(F32).astype(BF16), upper.astype(F32).astype(BF16))
    position = jnp.sum(jnp.where(named, count, 0.0), axis=0, keepdims=True).astype(jnp.int32) - 1
    slot = ids * cap + position
    half = local * cap
    place = lax.broadcasted_iota(jnp.int32, (2 * half, 1), 0)
    token = (lax.broadcasted_iota(jnp.int32, (EXTRA, rows), 1) // top + 1).astype(F32).astype(BF16)
    for k, out_ref in enumerate(out_refs):
        first = ((chip ^ k) * 2 + core) * half
        second = ((chip ^ k) * 2 + 1 - core) * half
        mine = jnp.where(place < half, place + first, place - half + second)
        onehot = (mine == slot).astype(F32).astype(BF16)
        out_ref[0:2 * half, :] = dot(onehot, act_ref[...]).astype(BF16)
        out_ref[2 * half:2 * half + EXTRA, :] = jnp.zeros((EXTRA, out_ref.shape[1]), BF16)
        out_ref[2 * half:2 * half + EXTRA, 0:2 * half] = dot(token, onehot, NT).astype(BF16)


def prep(ids_row, act, top, cap, local, chips):
    rows, width = act.shape
    shape = jax.ShapeDtypeStruct((2 * local * cap + EXTRA, width), BF16)
    return pl.pallas_call(
        functools.partial(prep_kernel, top, cap, local),
        out_shape=[shape] * chips,
        name="prep",
        compiler_params=pltpu.CompilerParams(vmem_limit_bytes=24 << 20),
        cost_estimate=pl.CostEstimate(
            flops=4 * rows * rows * width, bytes_accessed=4 * rows * width, transcendentals=0
        ),
    )(ids_row, act)


def selection(a_ref, groups_rows, tokens, start, width):
    named = a_ref[groups_rows:groups_rows + 1, 0:groups_rows].astype(F32)[:, start:start + width]
    return (lax.broadcasted_iota(jnp.int32, (tokens, 1), 0).astype(F32) + 1.0 == named).astype(F32).astype(BF16)


def token_grads_kernel(n, cap, local, *refs):
    a_refs, c_refs = refs[:n], refs[n:2 * n]
    up_refs, down_refs = refs[2 * n:2 * n + 2], refs[2 * n + 2:2 * n + 4]
    outs = refs[2 * n + 4:]
    part_refs, grad_rows_ref, cot_ref, slot_ref = outs[:n], outs[n], outs[n + 1], outs[n + 2]
    groups = 2 * local
    slots = groups * cap
    tokens = c_refs[0].shape[0]
    for k in range(n):
        pick = selection(a_refs[k], slots, tokens, 0, slots)
        rows = dot(pick, c_refs[k][...], TN).astype(BF16)
        for g in range(groups):
            cot_ref[g, k * cap:(k + 1) * cap, :] = rows[g * cap:(g + 1) * cap]
    for g in range(groups):
        grad_hidden = dot(cot_ref[g], down_refs[g // local][g % local], NT)
        act = jnp.concatenate([a_refs[k][g * cap:(g + 1) * cap, :] for k in range(n)], axis=0)
        grad_rows = (grad_hidden * act.astype(F32)).astype(BF16)
        grad_rows_ref[g] = grad_rows
        slot_grad = dot(grad_rows, up_refs[g // local][g % local], NT).astype(BF16)
        for k in range(n):
            slot_ref[k, g * cap:(g + 1) * cap, :] = slot_grad[k * cap:(k + 1) * cap]
    for k in range(n):
        pick = selection(a_refs[k], slots, tokens, 0, slots)
        part_refs[k][...] = dot(pick, slot_ref[k]).astype(BF16)


def token_grads(acts, cots, ups, downs, cap, local):
    n = len(acts)
    tokens, width = cots[0].shape
    hidden = ups[0].shape[2]
    groups = 2 * local
    outs = [jax.ShapeDtypeStruct((tokens, width), BF16)] * n + [
        jax.ShapeDtypeStruct((groups, n * cap, hidden), BF16),
        jax.ShapeDtypeStruct((groups, n * cap, width), BF16),
    ]
    result = pl.pallas_call(
        functools.partial(token_grads_kernel, n, cap, local),
        out_shape=outs,
        scratch_shapes=[pltpu.VMEM((n, groups * cap, width), BF16)],
        name="token_grads",
        compiler_params=pltpu.CompilerParams(vmem_limit_bytes=36 << 20),
        cost_estimate=pl.CostEstimate(
            flops=4 * groups * n * cap * hidden * width, bytes_accessed=24 << 20, transcendentals=0
        ),
    )(*acts, *cots, *ups, *downs)
    return result[:n], result[n], result[n + 1]


def weight_grads_kernel(n, cap, groups, group, added, *refs):
    a_refs, x_refs = refs[:n], refs[n:2 * n]
    up_ref, grad_rows_ref, cot_ref = refs[2 * n:2 * n + 3]
    more = refs[2 * n + 3:2 * n + 3 + 2 * added]
    grad_up_ref, grad_down_ref, x_ref = refs[-3:]
    tokens = x_refs[0].shape[0]
    for k in range(n):
        pick = selection(a_refs[k], groups * cap, tokens, group * cap, cap)
        x_ref[k * cap:(k + 1) * cap, :] = dot(pick, x_refs[k][...], TN).astype(BF16)
    act = jnp.concatenate([a_refs[k][group * cap:(group + 1) * cap, :] for k in range(n)], axis=0)
    hidden = (dot(x_ref[...], up_ref[0]) * act.astype(F32)).astype(BF16)
    grad_down = dot(hidden, cot_ref[0], TN)
    grad_up = dot(x_ref[...], grad_rows_ref[0], TN)
    if added:
        grad_up = grad_up + more[0][0].astype(F32)
        grad_down = grad_down + more[1][0].astype(F32)
    grad_down_ref[0] = grad_down.astype(BF16)
    grad_up_ref[0] = grad_up.astype(BF16)


def weight_grads(acts, xs, up, grad_rows, cot_rows, cap, group, more=(), total=1, into=()):
    n = len(acts)
    local, width, hidden = up.shape
    rows = n * cap
    mine = group if total > 1 else 0

    def whole(v):
        return pl.BlockSpec(v.shape, lambda i: (0,) * v.ndim)

    def one(v, j):
        return pl.BlockSpec((1, *v.shape[1:]), lambda i: (j, 0, 0))

    outs = [
        jax.ShapeDtypeStruct((total, width, hidden), BF16),
        jax.ShapeDtypeStruct((total, hidden, width), BF16),
    ]
    operands = (*acts, *xs, up, grad_rows, cot_rows, *more, *into)
    first = len(operands) - len(into)
    return pl.pallas_call(
        functools.partial(weight_grads_kernel, n, cap, 2 * local, group, len(more) // 2),
        grid=(1,),
        in_specs=[
            *[whole(v) for v in (*acts, *xs)],
            one(up, group % local),
            one(grad_rows, group),
            one(cot_rows, group),
            *[whole(v) for v in more],
            *[pl.BlockSpec(memory_space=pl.ANY) for _ in into],
        ],
        out_specs=[one(v, mine) for v in outs],
        out_shape=outs,
        input_output_aliases={first + i: i for i in range(len(into))},
        scratch_shapes=[pltpu.VMEM((rows, width), BF16)],
        compiler_params=pltpu.CompilerParams(vmem_limit_bytes=32 << 20),
        cost_estimate=pl.CostEstimate(
            flops=6 * rows * hidden * width, bytes_accessed=12 << 20, transcendentals=0
        ),
    )(*operands)


def body(inputs, upstream, gate_saved, expert_ids, route_weights, w_up, w_down):
    grid = Grid()
    local = w_up.shape[1]
    experts = local * grid.size
    tokens, top = expert_ids.shape[1:]
    hidden = w_up.shape[3]
    capacity = 3 * tokens * top // (2 * experts)
    cap = -(-capacity // 16) * 16
    zs, xs = grid.z, grid.x
    quads = zs == 4
    z_here = lax.axis_index("ep") // 2 // xs
    inner = (z_here == 1) | (z_here == 2)

    def along_z(d):
        return lambda z, x, core: (z ^ d, x, core)

    def along_x(d):
        return lambda z, x, core: (z, x ^ d, core)

    def across(z, x, core):
        return (z, x, 1 - core)

    def middle(z, x, core):
        return (3 - z, x, core) if z in (1, 2) else None

    def outward(z, x, core):
        return {1: (0, x, core), 2: (3, x, core)}.get(z)

    def inward(z, x, core):
        return {0: (1, x, core), 3: (2, x, core)}.get(z)

    def spread(block, far_block=None, side=False):
        rows = [block] + [None] * (zs - 1)
        if quads:
            rows[1] = grid.move(block, along_z(1))
            near = grid.move(block, middle)
            rows[2] = grid.move(block, along_z(2)) if far_block is None else far_block
            far = grid.move(rows[2], outward)
            rows[3] = jnp.where(inner, near, far)
        else:
            for d in range(1, zs):
                rows[d] = grid.move(block, along_z(d))
        blocks = []
        for z, row in enumerate(rows):
            blocks.append(row)
            for d in range(1, xs):
                if side and z == 1:
                    blocks.append(grid.move(blocks[d], along_z(1)))
                else:
                    blocks.append(grid.move(row, along_x(d)))
        return blocks

    cotangent = grid.move(upstream[0], along_z(0), -1)
    cot_far = grid.move(upstream[0], along_z(2), -1) if quads else None
    tokens_all = spread(inputs[0])

    scale = route_weights[0][:, :, None]
    act = (scale * jax.nn.silu(gate_saved[0].astype(F32))).astype(BF16)
    act = act.reshape(tokens * top, hidden)
    ids_row = expert_ids[0].reshape(1, tokens * top)
    blocks = prep(ids_row, act, top, cap, local, grid.chips)
    acts = [blocks[0]]
    for k in range(1, grid.chips):
        acts.append(grid.move(blocks[k], lambda z, x, core, k=k: (z ^ (k // xs), x ^ (k % xs), core)))

    cots = spread(cotangent, cot_far, quads)
    ups = (w_up[0], grid.move(w_up[0], across))
    downs = (w_down[0], grid.move(w_down[0], across))
    parts, grad_rows, cot_rows = token_grads(acts, cots, ups, downs, cap, local)

    def total(*values):
        return functools.reduce(jnp.add, [v.astype(F32) for v in values]).astype(BF16)

    rows = [None] * zs
    parts = list(parts)
    if quads:
        rows[1] = parts[xs]
        for d in range(1, xs):
            parts[d] = total(parts[d], grid.move(parts[xs + d], along_z(1)))
    for z in reversed(range(zs)):
        if rows[z] is None:
            arrived = [grid.move(parts[z * xs + d], along_x(d)) for d in range(1, xs)]
            rows[z] = total(parts[z * xs], *arrived)
    if quads:
        rows[2] = total(rows[2], grid.move(rows[3], inward))
        last = [grid.move(rows[3], middle, -1), grid.move(rows[2], along_z(2), -1), grid.move(rows[1], along_z(1), -1)]
    else:
        last = [grid.move(rows[d], along_z(d), -1) for d in range(1, zs)]
    last.append(grid.move(rows[0], along_z(0), -1))
    delivered = total(*last)[None]

    given = []
    for j in range(local):
        theirs = weight_grads(acts, tokens_all, ups[1], grad_rows, cot_rows, cap, local + j)
        given.append([grid.move(theirs[0], across), grid.move(theirs[1], across)])
    ours = ()
    for j in range(local):
        ours = weight_grads(acts, tokens_all, ups[0], grad_rows, cot_rows, cap, j, given[j], local, ours)
    grad_up, grad_down = ours
    return (delivered, grad_up[None], grad_down[None])


def solution(mesh):
    return jax.shard_map(
        body,
        mesh=mesh,
        in_specs=(
            P("section", "ep", None),
            P("section", "ep", None),
            P("section", "ep", None, None),
            P("section", "ep", None),
            P("section", "ep", None),
            P("section", "ep", None, None),
            P("section", "ep", None, None),
        ),
        out_specs=(
            P("section", "ep", None),
            P("section", "ep", None, None),
            P("section", "ep", None, None),
        ),
        check_vma=False,
    )
```

profile of v0, /device:TPU:10, one launch (start us, length us, event | category | flops | bytes accessed | tf_op | source)
XLA Modules:
  0.0 235.5 jit_solution(13350448266341365337)
XLA Ops:
  4.6 2.8 %prep.1 = (bf16[200,384]{1,0:T(8,128)(2,1)S(1)}, bf16[200,384]{1,0:T(8,128)(2,1)S(1)}, bf16[200,384]{1,0:T(8,128)(2,1)S(1)}, bf16[200,384]{1,0:T(8,128)(2,1)S(1)...) custom-call(s32[1,1024]{1,0:T(1,128)S(1)} %reshape_squeeze.3.ids_ref, ...), custom_call_target="tpu_custom_call" | custom-call | flops 1610612736 | bytes 1572864 | tf_op jit(solution)/shard_map/prep/pallas_call | solution.py:70
  8.6 3.0 %collective-permute-start.2 = (bf16[200,384]{1,0:T(8,128)(2,1)S(1)}, bf16[200,384]{1,0:T(8,128)(2,1)S(1)}, u32[]{:S(2)}, u32[]{:S(2)}) collective-permute-start(bf16[200,384]{1,0:T(8,128)(2,1)S(1)} %get-tuple-element.32), channel_id=1, source_target_pairs={{0,6},{1,7},{2,4},{3,5},{4,2},{5,3},{6,0},{7,1},{8,14},{9,15},{10,... | collective-permute-start | bytes 460808 | tf_op jit(solution)/shard_map/ppermute | solution.py:40
  11.6 2.5 %collective-permute-done.refs_1_ = bf16[200,384]{1,0:T(8,128)(2,1)S(1)} collective-permute-done((bf16[200,384]{1,0:T(8,128)(2,1)S(1)}, bf16[200,384]{1,0:T(8,128)(2,1)S(1)}, u32[]{:S(2)}, u32[]{:S(2)}) %collective-permute-start) | collective-permute-done | bytes 153632 | tf_op jit(solution)/shard_map/ppermute | solution.py:40
  14.7 3.5 %collective-permute-start.32 = (bf16[128,1536]{1,0:T(8,128)(2,1)S(1)}, bf16[128,1536]{1,0:T(8,128)(2,1)S(1)}, u32[]{:S(2)}, u32[]{:S(2)}) collective-permute-start(bf16[128,1536]{1,0:T(8,128)(2,1)S(1)} %bitcast.15), channel_id=1, source_target_pairs={{4,8},{5,9},{6,10},{7,11},{8,4},{9,5},{10,6},{11,7},{20,24},{21,25... | collective-permute-start | bytes 1179656 | tf_op jit(solution)/shard_map/ppermute | solution.py:40
  19.5 2.9 %collective-permute-start.4 = (bf16[200,384]{1,0:T(8,128)(2,1)S(1)}, bf16[200,384]{1,0:T(8,128)(2,1)S(1)}, u32[]{:S(2)}, u32[]{:S(2)}) collective-permute-start(bf16[200,384]{1,0:T(8,128)(2,1)S(1)} %get-tuple-element.34), channel_id=1, source_target_pairs={{0,10},{1,11},{2,8},{3,9},{4,14},{5,15},{6,12},{7,13},{8,2},{9,3},... | collective-permute-start | bytes 460808 | tf_op jit(solution)/shard_map/ppermute | solution.py:40
  22.4 15.1 %collective-permute-done.3.refs_4_ = bf16[200,384]{1,0:T(8,128)(2,1)S(1)} collective-permute-done((bf16[200,384]{1,0:T(8,128)(2,1)S(1)}, bf16[200,384]{1,0:T(8,128)(2,1)S(1)}, u32[]{:S(2)}, u32[]{:S(2)}) %collective-permute-start.3) | collective-permute-done | bytes 153632 | tf_op jit(solution)/shard_map/ppermute | solution.py:40
  38.7 3.8 %collective-permute-done.4.refs_5_ = bf16[200,384]{1,0:T(8,128)(2,1)S(1)} collective-permute-done((bf16[200,384]{1,0:T(8,128)(2,1)S(1)}, bf16[200,384]{1,0:T(8,128)(2,1)S(1)}, u32[]{:S(2)}, u32[]{:S(2)}) %collective-permute-start.4) | collective-permute-done | bytes 153632 | tf_op jit(solution)/shard_map/ppermute | solution.py:40
  43.6 12.3 %collective-permute-done.5.refs_6_ = bf16[200,384]{1,0:T(8,128)(2,1)S(1)} collective-permute-done((bf16[200,384]{1,0:T(8,128)(2,1)S(1)}, bf16[200,384]{1,0:T(8,128)(2,1)S(1)}, u32[]{:S(2)}, u32[]{:S(2)}) %collective-permute-start.5) | collective-permute-done | bytes 153632 | tf_op jit(solution)/shard_map/ppermute | solution.py:40
  56.5 2.6 %collective-permute-done.6.refs_7_ = bf16[200,384]{1,0:T(8,128)(2,1)S(1)} collective-permute-done((bf16[200,384]{1,0:T(8,128)(2,1)S(1)}, bf16[200,384]{1,0:T(8,128)(2,1)S(1)}, u32[]{:S(2)}, u32[]{:S(2)}) %collective-permute-start.6) | collective-permute-done | bytes 153632 | tf_op jit(solution)/shard_map/ppermute | solution.py:40
  61.6 17.7 %collective-permute-done.30.refs_12_ = bf16[128,1536]{1,0:T(8,128)(2,1)S(1)} collective-permute-done((bf16[128,1536]{1,0:T(8,128)(2,1)S(1)}, bf16[128,1536]{1,0:T(8,128)(2,1)S(1)}, u32[]{:S(2)}, u32[]{:S(2)}) %collective-permute-start.30) | collective-permute-done | bytes 393248 | tf_op jit(solution)/shard_map/ppermute | solution.py:40
  79.3 2.9 %collective-permute-start.28 = (bf16[128,1536]{1,0:T(8,128)(2,1)S(1)}, bf16[128,1536]{1,0:T(8,128)(2,1)S(1)}, u32[]{:S(2)}, u32[]{:S(2)}) collective-permute-start(bf16[128,1536]{1,0:T(8,128)(2,1)S(1)} %bitcast.17), channel_id=1, source_target_pairs={{0,4},{1,5},{2,6},{3,7},{4,0},{5,1},{6,2},{7,3},{8,12},{9,13},{10,... | collective-permute-start | bytes 1179656 | tf_op jit(solution)/shard_map/ppermute | solution.py:40
  82.3 3.8 %collective-permute-done.11.refs_12_ = bf16[128,1536]{1,0:T(8,128)(2,1)} collective-permute-done((bf16[128,1536]{1,0:T(8,128)(2,1)S(1)}, bf16[128,1536]{1,0:T(8,128)(2,1)}, u32[]{:S(2)}, u32[]{:S(2)}) %collective-permute-start.11) | collective-permute-done | bytes 393248 | tf_op jit(solution)/shard_map/ppermute | solution.py:40
  86.0 6.1 %collective-permute-start.14 = (bf16[128,1536]{1,0:T(8,128)(2,1)}, bf16[128,1536]{1,0:T(8,128)(2,1)}, u32[]{:S(2)}, u32[]{:S(2)}) collective-permute-start(bf16[128,1536]{1,0:T(8,128)(2,1)} %collective-permute-done.11.refs_12_), channel_id=1, source_target_pairs={{4,0},{5,1},{6,2},{7,3},{8,12},{9,13},{10,14},{11,15},{20,16},{21,... | collective-permute-start | bytes 1179656 | tf_op jit(solution)/shard_map/ppermute | solution.py:40
  92.2 3.5 %collective-permute-start.13 = (bf16[128,1536]{1,0:T(8,128)(2,1)}, bf16[128,1536]{1,0:T(8,128)(2,1)}, u32[]{:S(2)}, u32[]{:S(2)}) collective-permute-start(bf16[128,1536]{1,0:T(8,128)(2,1)} %collective-permute-done.7.refs_8_), channel_id=1, source_target_pairs={{4,8},{5,9},{6,10},{7,11},{8,4},{9,5},{10,6},{11,7},{20,24},{21,25... | collective-permute-start | bytes 1179656 | tf_op jit(solution)/shard_map/ppermute | solution.py:40
  96.3 6.5 %collective-permute-done.14 = bf16[128,1536]{1,0:T(8,128)(2,1)} collective-permute-done((bf16[128,1536]{1,0:T(8,128)(2,1)}, bf16[128,1536]{1,0:T(8,128)(2,1)}, u32[]{:S(2)}, u32[]{:S(2)}) %collective-permute-start.14) | collective-permute-done | bytes 393248 | tf_op jit(solution)/shard_map/ppermute | solution.py:40
  103.4 4.6 %collective-permute-start.33 = (bf16[128,1536]{1,0:T(8,128)(2,1)S(1)}, bf16[128,1536]{1,0:T(8,128)(2,1)S(1)}, u32[]{:S(2)}, u32[]{:S(2)}) collective-permute-start(bf16[128,1536]{1,0:T(8,128)(2,1)S(1)} %collective-permute-done.30.refs_12_), channel_id=1, source_target_pairs={{4,0},{5,1},{6,2},{7,3},{8,12},{9,13},{10,14},{11,15},{20,16},{21,... | collective-permute-start | bytes 1179656 | tf_op jit(solution)/shard_map/ppermute | solution.py:40
  109.0 7.0 %collective-permute-done.33 = bf16[128,1536]{1,0:T(8,128)(2,1)S(1)} collective-permute-done((bf16[128,1536]{1,0:T(8,128)(2,1)S(1)}, bf16[128,1536]{1,0:T(8,128)(2,1)S(1)}, u32[]{:S(2)}, u32[]{:S(2)}) %collective-permute-start.33) | collective-permute-done | bytes 393248 | tf_op jit(solution)/shard_map/ppermute | solution.py:40
  116.0 2.5 %collective-permute-start.9 = (bf16[128,1536]{1,0:T(8,128)(2,1)}, bf16[128,1536]{1,0:T(8,128)(2,1)S(1)}, u32[]{:S(2)}, u32[]{:S(2)}) collective-permute-start(bf16[128,1536]{1,0:T(8,128)(2,1)} %collective-permute-done.7.refs_8_), channel_id=1, source_target_pairs={{0,4},{1,5},{2,6},{3,7},{4,0},{5,1},{6,2},{7,3},{8,12},{9,13},{10,... | collective-permute-start | bytes 1179656 | tf_op jit(solution)/shard_map/ppermute | solution.py:40
  121.0 7.6 %collective-permute-done.9.refs_10_ = bf16[128,1536]{1,0:T(8,128)(2,1)S(1)} collective-permute-done((bf16[128,1536]{1,0:T(8,128)(2,1)}, bf16[128,1536]{1,0:T(8,128)(2,1)S(1)}, u32[]{:S(2)}, u32[]{:S(2)}) %collective-permute-start.9) | collective-permute-done | bytes 393248 | tf_op jit(solution)/shard_map/ppermute | solution.py:40
  130.7 4.6 %collective-permute-done.10.refs_11_ = bf16[128,1536]{1,0:T(8,128)(2,1)S(1)} collective-permute-done((bf16[128,1536]{1,0:T(8,128)(2,1)S(1)}, bf16[128,1536]{1,0:T(8,128)(2,1)S(1)}, u32[]{:S(2)}, u32[]{:S(2)}) %collective-permute-start.10) | collective-permute-done | bytes 393248 | tf_op jit(solution)/shard_map/ppermute | solution.py:40
  146.3 12.2 %token_grads.1 = (bf16[128,1536]{1,0:T(8,128)(2,1)S(1)}, bf16[128,1536]{1,0:T(8,128)(2,1)S(1)}, bf16[128,1536]{1,0:T(8,128)(2,1)S(1)}, bf16[128,1536]{1,0:T(8,12...) custom-call(bf16[200,384]{1,0:T(8,128)(2,1)S(1)} %copy-done.4, ...), custom_call_target="tpu_custom_call" | custom-call | flops 3623878656 | bytes 25165824 | tf_op jit(solution)/shard_map/token_grads/pallas_call | solution.py:121
  160.5 2.7 %collective-permute-start.23 = (bf16[128,1536]{1,0:T(8,128)(2,1)S(1)}, bf16[128,1536]{1,0:T(8,128)(2,1)S(1)}, u32[]{:S(2)}, u32[]{:S(2)}) collective-permute-start(bf16[128,1536]{1,0:T(8,128)(2,1)S(1)} %get-tuple-element.41), channel_id=1, source_target_pairs={{0,20},{1,21},{2,22},{3,23},{4,16},{5,17},{6,18},{7,19},{8,28},{9,... | collective-permute-start | bytes 1179656 | tf_op jit(solution)/shard_map/ppermute | solution.py:40
  164.9 2.3 copy-done
  167.2 4.5 %shard_map.95 = (bf16[1,1536,384]{2,1,0:T(8,128)(2,1)S(1)}, bf16[1,384,1536]{2,1,0:T(8,128)(2,1)S(1)}) custom-call(bf16[200,384]{1,0:T(8,128)(2,1)S(1)} %copy-done.4, bf16[200,384]{1,0:T(8,128)(2,1)S(1)} %copy-done.6, bf16[200,384]{1,0:T(8,128)(2,1)S(1)} %copy-done.8, bf16[200,384]{1,0:T(8,128)(2,1)S(1)} %copy-done.11, bf16[200,384]{1,0:T(8,128)(2,1)S(1)} %copy-done.14, ...), custom_call_target="tpu_custom_call" | custom-call | flops 1358954496 | bytes 12582912 | tf_op jit(solution)/shard_map/pallas_call | solution.py:172
  171.8 4.2 %shard_map.94 = (bf16[1,1536,384]{2,1,0:T(8,128)(2,1)S(1)}, bf16[1,384,1536]{2,1,0:T(8,128)(2,1)S(1)}) custom-call(bf16[200,384]{1,0:T(8,128)(2,1)S(1)} %copy-done.4, bf16[200,384]{1,0:T(8,128)(2,1)S(1)} %copy-done.6, bf16[200,384]{1,0:T(8,128)(2,1)S(1)} %copy-done.8, bf16[200,384]{1,0:T(8,128)(2,1)S(1)} %copy-done.11, bf16[200,384]{1,0:T(8,128)(2,1)S(1)} %copy-done.14, ...), custom_call_target="tpu_custom_call" | custom-call | flops 1358954496 | bytes 12582912 | tf_op jit(solution)/shard_map/pallas_call | solution.py:172
  179.8 10.1 %collective-permute-done.21 = bf16[128,1536]{1,0:T(8,128)(2,1)S(1)} collective-permute-done((bf16[128,1536]{1,0:T(8,128)(2,1)S(1)}, bf16[128,1536]{1,0:T(8,128)(2,1)S(1)}, u32[]{:S(2)}, u32[]{:S(2)}) %collective-permute-start.21) | collective-permute-done | bytes 393248 | tf_op jit(solution)/shard_map/ppermute | solution.py:40
  191.5 7.1 %collective-permute-done.25 = bf16[128,1536]{1,0:T(8,128)(2,1)S(1)} collective-permute-done((bf16[128,1536]{1,0:T(8,128)(2,1)S(1)}, bf16[128,1536]{1,0:T(8,128)(2,1)S(1)}, u32[]{:S(2)}, u32[]{:S(2)}) %collective-permute-start.25) | collective-permute-done | bytes 393248 | tf_op jit(solution)/shard_map/ppermute | solution.py:40
  198.7 5.5 %collective-permute-start.19 = (bf16[128,1536]{1,0:T(8,128)(2,1)S(1)}, bf16[128,1536]{1,0:T(8,128)(2,1)S(1)}, u32[]{:S(2)}, u32[]{:S(2)}) collective-permute-start(bf16[128,1536]{1,0:T(8,128)(2,1)S(1)} %add_convert_fusion.5), channel_id=1, source_target_pairs={{4,24},{5,25},{6,26},{7,27},{8,20},{9,21},{10,22},{11,23},{20,8},{... | collective-permute-start | bytes 1179656 | tf_op jit(solution)/shard_map/ppermute | solution.py:40
  204.4 3.6 %shard_map.96 = (bf16[2,1536,384]{2,1,0:T(8,128)(2,1)}, bf16[2,384,1536]{2,1,0:T(8,128)(2,1)}) custom-call(bf16[200,384]{1,0:T(8,128)(2,1)S(1)} %copy-done.4, bf16[200,384]{1,0:T(8,128)(2,1)S(1)} %copy-done.6, bf16[200,384]{1,0:T(8,128)(2,1)S(1)} %copy-done.8, bf16[200,384]{1,0:T(8,128)(2,1)S(1)} %copy-done.11, bf16[200,384]{1,0:T(8,128)(2,1)S(1)} %copy-done.14, ...), custom_call_target="tpu_custom_call" | custom-call | flops 1358954496 | bytes 12582912 | tf_op jit(solution)/shard_map/pallas_call | solution.py:172
  208.0 14.6 %collective-permute-done.19 = bf16[128,1536]{1,0:T(8,128)(2,1)S(1)} collective-permute-done((bf16[128,1536]{1,0:T(8,128)(2,1)S(1)}, bf16[128,1536]{1,0:T(8,128)(2,1)S(1)}, u32[]{:S(2)}, u32[]{:S(2)}) %collective-permute-start.19) | collective-permute-done | bytes 393248 | tf_op jit(solution)/shard_map/ppermute | solution.py:40
  222.6 7.5 %collective-permute-done.22 = bf16[128,1536]{1,0:T(8,128)(2,1)S(1)} collective-permute-done((bf16[128,1536]{1,0:T(8,128)(2,1)S(1)}, bf16[128,1536]{1,0:T(8,128)(2,1)S(1)}, u32[]{:S(2)}, u32[]{:S(2)}) %collective-permute-start.22) | collective-permute-done | bytes 393248 | tf_op jit(solution)/shard_map/ppermute | solution.py:40
  231.8 3.7 %shard_map.97 = (bf16[2,1536,384]{2,1,0:T(8,128)(2,1)}, bf16[2,384,1536]{2,1,0:T(8,128)(2,1)}) custom-call(bf16[200,384]{1,0:T(8,128)(2,1)S(1)} %copy-done.4, bf16[200,384]{1,0:T(8,128)(2,1)S(1)} %copy-done.6, bf16[200,384]{1,0:T(8,128)(2,1)S(1)} %copy-done.8, bf16[200,384]{1,0:T(8,128)(2,1)S(1)} %copy-done.11, ...), custom_call_target="tpu_custom_call", output_to_operand_aliasing={{0}: (21, {}), {1}: (22, {})} | custom-call | flops 1358954496 | bytes 12582912 | tf_op jit(solution)/shard_map/pallas_call | solution.py:172
  (118 shorter events, 41.2 us)
Async XLA Ops:
  0.6 136.2 %collective-permute-start.16 = (bf16[2,1536,384]{2,1,0:T(8,128)(2,1)}, bf16[2,1536,384]{2,1,0:T(8,128)(2,1)}, u32[]{:S(2)}, u32[]{:S(2)}) collective-permute-start(bf16[2,1536,384]{2,1,0:T(8,128)(2,1)} %bitcast.11), channel_id=1, source_target_pairs={{0,1},{1,0},{2,3},{3,2},{4,5},{5,4},{6,7},{7,6},{8,9},{9,8},{10,11... | collective-permute-start | bytes 7077896 | tf_op jit(solution)/shard_map/ppermute | solution.py:40
  0.7 136.6 %collective-permute-start.17 = (bf16[2,384,1536]{2,1,0:T(8,128)(2,1)}, bf16[2,384,1536]{2,1,0:T(8,128)(2,1)}, u32[]{:S(2)}, u32[]{:S(2)}) collective-permute-start(bf16[2,384,1536]{2,1,0:T(8,128)(2,1)} %bitcast.23), channel_id=1, source_target_pairs={{0,1},{1,0},{2,3},{3,2},{4,5},{5,4},{6,7},{7,6},{8,9},{9,8},{10,11... | collective-permute-start | bytes 7077896 | tf_op jit(solution)/shard_map/ppermute | solution.py:40
  14.7 46.3 %collective-permute-start.32 = (bf16[128,1536]{1,0:T(8,128)(2,1)S(1)}, bf16[128,1536]{1,0:T(8,128)(2,1)S(1)}, u32[]{:S(2)}, u32[]{:S(2)}) collective-permute-start(bf16[128,1536]{1,0:T(8,128)(2,1)S(1)} %bitcast.15), channel_id=1, source_target_pairs={{4,8},{5,9},{6,10},{7,11},{8,4},{9,5},{10,6},{11,7},{20,24},{21,25... | collective-permute-start | bytes 1179656 | tf_op jit(solution)/shard_map/ppermute | solution.py:40
  18.9 18.7 %collective-permute-start.3 = (bf16[200,384]{1,0:T(8,128)(2,1)S(1)}, bf16[200,384]{1,0:T(8,128)(2,1)S(1)}, u32[]{:S(2)}, u32[]{:S(2)}) collective-permute-start(bf16[200,384]{1,0:T(8,128)(2,1)S(1)} %get-tuple-element.33), channel_id=1, source_target_pairs={{0,8},{1,9},{2,10},{3,11},{4,12},{5,13},{6,14},{7,15},{8,0},{9,1},... | collective-permute-start | bytes 460808 | tf_op jit(solution)/shard_map/ppermute | solution.py:40
  19.5 23.0 %collective-permute-start.4 = (bf16[200,384]{1,0:T(8,128)(2,1)S(1)}, bf16[200,384]{1,0:T(8,128)(2,1)S(1)}, u32[]{:S(2)}, u32[]{:S(2)}) collective-permute-start(bf16[200,384]{1,0:T(8,128)(2,1)S(1)} %get-tuple-element.34), channel_id=1, source_target_pairs={{0,10},{1,11},{2,8},{3,9},{4,14},{5,15},{6,12},{7,13},{8,2},{9,3},... | collective-permute-start | bytes 460808 | tf_op jit(solution)/shard_map/ppermute | solution.py:40
  38.2 17.6 %collective-permute-start.5 = (bf16[200,384]{1,0:T(8,128)(2,1)S(1)}, bf16[200,384]{1,0:T(8,128)(2,1)S(1)}, u32[]{:S(2)}, u32[]{:S(2)}) collective-permute-start(bf16[200,384]{1,0:T(8,128)(2,1)S(1)} %get-tuple-element.35), channel_id=1, source_target_pairs={{0,12},{1,13},{2,14},{3,15},{4,8},{5,9},{6,10},{7,11},{8,4},{9,5},... | collective-permute-start | bytes 460808 | tf_op jit(solution)/shard_map/ppermute | solution.py:40
  43.2 16.0 %collective-permute-start.6 = (bf16[200,384]{1,0:T(8,128)(2,1)S(1)}, bf16[200,384]{1,0:T(8,128)(2,1)S(1)}, u32[]{:S(2)}, u32[]{:S(2)}) collective-permute-start(bf16[200,384]{1,0:T(8,128)(2,1)S(1)} %get-tuple-element.36), channel_id=1, source_target_pairs={{0,14},{1,15},{2,12},{3,13},{4,10},{5,11},{6,8},{7,9},{8,6},{9,7},... | collective-permute-start | bytes 460808 | tf_op jit(solution)/shard_map/ppermute | solution.py:40
  56.5 22.8 %collective-permute-start.30 = (bf16[128,1536]{1,0:T(8,128)(2,1)S(1)}, bf16[128,1536]{1,0:T(8,128)(2,1)S(1)}, u32[]{:S(2)}, u32[]{:S(2)}) collective-permute-start(bf16[128,1536]{1,0:T(8,128)(2,1)S(1)} %bitcast.16), channel_id=1, source_target_pairs={{0,8},{1,9},{2,10},{3,11},{4,12},{5,13},{6,14},{7,15},{8,0},{9,1},... | collective-permute-start | bytes 1179656 | tf_op jit(solution)/shard_map/ppermute | solution.py:40
  59.8 26.3 %collective-permute-start.11 = (bf16[128,1536]{1,0:T(8,128)(2,1)S(1)}, bf16[128,1536]{1,0:T(8,128)(2,1)}, u32[]{:S(2)}, u32[]{:S(2)}) collective-permute-start(bf16[128,1536]{1,0:T(8,128)(2,1)S(1)} %bitcast.27), channel_id=1, source_target_pairs={{0,24},{1,25},{2,26},{3,27},{4,28},{5,29},{6,30},{7,31},{8,16},{9,... | collective-permute-start | bytes 1179656 | tf_op jit(solution)/shard_map/ppermute | solution.py:40
  61.1 31.1 %collective-permute-start.7 = (bf16[128,1536]{1,0:T(8,128)(2,1)S(1)}, bf16[128,1536]{1,0:T(8,128)(2,1)}, u32[]{:S(2)}, u32[]{:S(2)}) collective-permute-start(bf16[128,1536]{1,0:T(8,128)(2,1)S(1)} %bitcast.28), channel_id=1, source_target_pairs={{0,16},{1,17},{2,18},{3,19},{4,20},{5,21},{6,22},{7,23},{8,24},{9,... | collective-permute-start | bytes 1179656 | tf_op jit(solution)/shard_map/ppermute | solution.py:40
  79.3 16.4 %collective-permute-start.28 = (bf16[128,1536]{1,0:T(8,128)(2,1)S(1)}, bf16[128,1536]{1,0:T(8,128)(2,1)S(1)}, u32[]{:S(2)}, u32[]{:S(2)}) collective-permute-start(bf16[128,1536]{1,0:T(8,128)(2,1)S(1)} %bitcast.17), channel_id=1, source_target_pairs={{0,4},{1,5},{2,6},{3,7},{4,0},{5,1},{6,2},{7,3},{8,12},{9,13},{10,... | collective-permute-start | bytes 1179656 | tf_op jit(solution)/shard_map/ppermute | solution.py:40
  86.0 16.8 %collective-permute-start.14 = (bf16[128,1536]{1,0:T(8,128)(2,1)}, bf16[128,1536]{1,0:T(8,128)(2,1)}, u32[]{:S(2)}, u32[]{:S(2)}) collective-permute-start(bf16[128,1536]{1,0:T(8,128)(2,1)} %collective-permute-done.11.refs_12_), channel_id=1, source_target_pairs={{4,0},{5,1},{6,2},{7,3},{8,12},{9,13},{10,14},{11,15},{20,16},{21,... | collective-permute-start | bytes 1179656 | tf_op jit(solution)/shard_map/ppermute | solution.py:40
  95.7 22.8 %collective-permute-start.12 = (bf16[128,1536]{1,0:T(8,128)(2,1)}, bf16[128,1536]{1,0:T(8,128)(2,1)S(1)}, u32[]{:S(2)}, u32[]{:S(2)}) collective-permute-start(bf16[128,1536]{1,0:T(8,128)(2,1)} %collective-permute-done.11.refs_12_), channel_id=1, source_target_pairs={{0,2},{1,3},{2,0},{3,1},{4,6},{5,7},{6,4},{7,5},{8,10},{9,11},{10,... | collective-permute-start | bytes 1179656 | tf_op jit(solution)/shard_map/ppermute | solution.py:40
  102.8 17.2 %collective-permute-start.8 = (bf16[128,1536]{1,0:T(8,128)(2,1)}, bf16[128,1536]{1,0:T(8,128)(2,1)S(1)}, u32[]{:S(2)}, u32[]{:S(2)}) collective-permute-start(bf16[128,1536]{1,0:T(8,128)(2,1)} %collective-permute-done.7.refs_8_), channel_id=1, source_target_pairs={{0,2},{1,3},{2,0},{3,1},{4,6},{5,7},{6,4},{7,5},{8,10},{9,11},{10,... | collective-permute-start | bytes 1179656 | tf_op jit(solution)/shard_map/ppermute | solution.py:40
  103.4 12.6 %collective-permute-start.33 = (bf16[128,1536]{1,0:T(8,128)(2,1)S(1)}, bf16[128,1536]{1,0:T(8,128)(2,1)S(1)}, u32[]{:S(2)}, u32[]{:S(2)}) collective-permute-start(bf16[128,1536]{1,0:T(8,128)(2,1)S(1)} %collective-permute-done.30.refs_12_), channel_id=1, source_target_pairs={{4,0},{5,1},{6,2},{7,3},{8,12},{9,13},{10,14},{11,15},{20,16},{21,... | collective-permute-start | bytes 1179656 | tf_op jit(solution)/shard_map/ppermute | solution.py:40
  116.0 12.7 %collective-permute-start.9 = (bf16[128,1536]{1,0:T(8,128)(2,1)}, bf16[128,1536]{1,0:T(8,128)(2,1)S(1)}, u32[]{:S(2)}, u32[]{:S(2)}) collective-permute-start(bf16[128,1536]{1,0:T(8,128)(2,1)} %collective-permute-done.7.refs_8_), channel_id=1, source_target_pairs={{0,4},{1,5},{2,6},{3,7},{4,0},{5,1},{6,2},{7,3},{8,12},{9,13},{10,... | collective-permute-start | bytes 1179656 | tf_op jit(solution)/shard_map/ppermute | solution.py:40
  120.0 15.3 %collective-permute-start.10 = (bf16[128,1536]{1,0:T(8,128)(2,1)S(1)}, bf16[128,1536]{1,0:T(8,128)(2,1)S(1)}, u32[]{:S(2)}, u32[]{:S(2)}) collective-permute-start(bf16[128,1536]{1,0:T(8,128)(2,1)S(1)} %collective-permute-done.8.refs_9_), channel_id=1, source_target_pairs={{0,4},{1,5},{2,6},{3,7},{4,0},{5,1},{6,2},{7,3},{8,12},{9,13},{10,... | collective-permute-start | bytes 1179656 | tf_op jit(solution)/shard_map/ppermute | solution.py:40
  128.7 31.3 %collective-permute-start.27 = (bf16[128,1536]{1,0:T(8,128)(2,1)S(1)}, bf16[128,1536]{1,0:T(8,128)(2,1)S(1)}, u32[]{:S(2)}, u32[]{:S(2)}) collective-permute-start(bf16[128,1536]{1,0:T(8,128)(2,1)S(1)} %bitcast.18), channel_id=1, source_target_pairs={{0,2},{1,3},{2,0},{3,1},{4,6},{5,7},{6,4},{7,5},{8,10},{9,11},{10,... | collective-permute-start | bytes 1179656 | tf_op jit(solution)/shard_map/ppermute | solution.py:40
  130.2 30.3 %collective-permute-start.31 = (bf16[128,1536]{1,0:T(8,128)(2,1)S(1)}, bf16[128,1536]{1,0:T(8,128)(2,1)S(1)}, u32[]{:S(2)}, u32[]{:S(2)}) collective-permute-start(bf16[128,1536]{1,0:T(8,128)(2,1)S(1)} %collective-permute-done.30.refs_12_), channel_id=1, source_target_pairs={{0,2},{1,3},{2,0},{3,1},{4,6},{5,7},{6,4},{7,5},{8,10},{9,11},{10,... | collective-permute-start | bytes 1179656 | tf_op jit(solution)/shard_map/ppermute | solution.py:40
  135.3 27.9 %collective-permute-start.29 = (bf16[128,1536]{1,0:T(8,128)(2,1)S(1)}, bf16[128,1536]{1,0:T(8,128)(2,1)S(1)}, u32[]{:S(2)}, u32[]{:S(2)}) collective-permute-start(bf16[128,1536]{1,0:T(8,128)(2,1)S(1)} %collective-permute-done.28.refs_10_), channel_id=1, source_target_pairs={{0,2},{1,3},{2,0},{3,1},{4,6},{5,7},{6,4},{7,5},{8,10},{9,11},{10,... | collective-permute-start | bytes 1179656 | tf_op jit(solution)/shard_map/ppermute | solution.py:40
  136.8 28.1 %collective-permute-start.34 = (bf16[128,1536]{1,0:T(8,128)(2,1)S(1)}, bf16[128,1536]{1,0:T(8,128)(2,1)S(1)}, u32[]{:S(2)}, u32[]{:S(2)}) collective-permute-start(bf16[128,1536]{1,0:T(8,128)(2,1)S(1)} %broadcast_select_fusion.refs_14_), channel_id=1, source_target_pairs={{0,2},{1,3},{2,0},{3,1},{4,6},{5,7},{6,4},{7,5},{8,10},{9,11},{10,... | collective-permute-start | bytes 1179656 | tf_op jit(solution)/shard_map/ppermute | solution.py:40
  158.5 17.5 %collective-permute-start.18 = (bf16[128,1536]{1,0:T(8,128)(2,1)S(1)}, bf16[128,1536]{1,0:T(8,128)(2,1)S(1)}, u32[]{:S(2)}, u32[]{:S(2)}) collective-permute-start(bf16[128,1536]{1,0:T(8,128)(2,1)S(1)} %get-tuple-element.38), channel_id=1, source_target_pairs={{0,2},{1,3},{2,0},{3,1},{4,6},{5,7},{6,4},{7,5},{8,10},{9,11},{10,... | collective-permute-start | bytes 1179656 | tf_op jit(solution)/shard_map/ppermute | solution.py:40
  160.0 19.7 %collective-permute-start.20 = (bf16[128,1536]{1,0:T(8,128)(2,1)S(1)}, bf16[128,1536]{1,0:T(8,128)(2,1)S(1)}, u32[]{:S(2)}, u32[]{:S(2)}) collective-permute-start(bf16[128,1536]{1,0:T(8,128)(2,1)S(1)} %get-tuple-element.40), channel_id=1, source_target_pairs={{0,2},{1,3},{2,0},{3,1},{4,6},{5,7},{6,4},{7,5},{8,10},{9,11},{10,... | collective-permute-start | bytes 1179656 | tf_op jit(solution)/shard_map/ppermute | solution.py:40
  160.5 38.2 %collective-permute-start.23 = (bf16[128,1536]{1,0:T(8,128)(2,1)S(1)}, bf16[128,1536]{1,0:T(8,128)(2,1)S(1)}, u32[]{:S(2)}, u32[]{:S(2)}) collective-permute-start(bf16[128,1536]{1,0:T(8,128)(2,1)S(1)} %get-tuple-element.41), channel_id=1, source_target_pairs={{0,20},{1,21},{2,22},{3,23},{4,16},{5,17},{6,18},{7,19},{8,28},{9,... | collective-permute-start | bytes 1179656 | tf_op jit(solution)/shard_map/ppermute | solution.py:40
  163.2 14.9 %collective-permute-start.24 = (bf16[128,1536]{1,0:T(8,128)(2,1)S(1)}, bf16[128,1536]{1,0:T(8,128)(2,1)S(1)}, u32[]{:S(2)}, u32[]{:S(2)}) collective-permute-start(bf16[128,1536]{1,0:T(8,128)(2,1)S(1)} %get-tuple-element.44), channel_id=1, source_target_pairs={{0,4},{1,5},{2,6},{3,7},{4,0},{5,1},{6,2},{7,3},{8,12},{9,13},{10,... | collective-permute-start | bytes 1179656 | tf_op jit(solution)/shard_map/ppermute | solution.py:40
  171.7 32.5 %collective-permute-start.37 = (bf16[1,1536,384]{2,1,0:T(8,128)(2,1)S(1)}, bf16[1,1536,384]{2,1,0:T(8,128)(2,1)S(1)}, u32[]{:S(2)}, u32[]{:S(2)}) collective-permute-start(bf16[1,1536,384]{2,1,0:T(8,128)(2,1)S(1)} %get-tuple-element.49), channel_id=1, source_target_pairs={{0,1},{1,0},{2,3},{3,2},{4,5},{5,4},{6,7},{7,6},{8,9},{9,8},{10,11... | collective-permute-start | bytes 3538952 | tf_op jit(solution)/shard_map/ppermute | solution.py:40
  176.0 28.3 %collective-permute-start.38 = (bf16[1,384,1536]{2,1,0:T(8,128)(2,1)S(1)}, bf16[1,384,1536]{2,1,0:T(8,128)(2,1)S(1)}, u32[]{:S(2)}, u32[]{:S(2)}) collective-permute-start(bf16[1,384,1536]{2,1,0:T(8,128)(2,1)S(1)} %get-tuple-element.50), channel_id=1, source_target_pairs={{0,1},{1,0},{2,3},{3,2},{4,5},{5,4},{6,7},{7,6},{8,9},{9,8},{10,11... | collective-permute-start | bytes 3538952 | tf_op jit(solution)/shard_map/ppermute | solution.py:40
  179.7 52.1 %collective-permute-start.35 = (bf16[1,1536,384]{2,1,0:T(8,128)(2,1)S(1)}, bf16[1,1536,384]{2,1,0:T(8,128)(2,1)S(1)}, u32[]{:S(2)}, u32[]{:S(2)}) collective-permute-start(bf16[1,1536,384]{2,1,0:T(8,128)(2,1)S(1)} %get-tuple-element.47), channel_id=1, source_target_pairs={{0,1},{1,0},{2,3},{3,2},{4,5},{5,4},{6,7},{7,6},{8,9},{9,8},{10,11... | collective-permute-start | bytes 3538952 | tf_op jit(solution)/shard_map/ppermute | solution.py:40
  198.6 33.1 %collective-permute-start.36 = (bf16[1,384,1536]{2,1,0:T(8,128)(2,1)S(1)}, bf16[1,384,1536]{2,1,0:T(8,128)(2,1)S(1)}, u32[]{:S(2)}, u32[]{:S(2)}) collective-permute-start(bf16[1,384,1536]{2,1,0:T(8,128)(2,1)S(1)} %get-tuple-element.48), channel_id=1, source_target_pairs={{0,1},{1,0},{2,3},{3,2},{4,5},{5,4},{6,7},{7,6},{8,9},{9,8},{10,11... | collective-permute-start | bytes 3538952 | tf_op jit(solution)/shard_map/ppermute | solution.py:40
  198.7 23.9 %collective-permute-start.19 = (bf16[128,1536]{1,0:T(8,128)(2,1)S(1)}, bf16[128,1536]{1,0:T(8,128)(2,1)S(1)}, u32[]{:S(2)}, u32[]{:S(2)}) collective-permute-start(bf16[128,1536]{1,0:T(8,128)(2,1)S(1)} %add_convert_fusion.5), channel_id=1, source_target_pairs={{4,24},{5,25},{6,26},{7,27},{8,20},{9,21},{10,22},{11,23},{20,8},{... | collective-permute-start | bytes 1179656 | tf_op jit(solution)/shard_map/ppermute | solution.py:40
  204.2 25.9 %collective-permute-start.22 = (bf16[128,1536]{1,0:T(8,128)(2,1)S(1)}, bf16[128,1536]{1,0:T(8,128)(2,1)S(1)}, u32[]{:S(2)}, u32[]{:S(2)}) collective-permute-start(bf16[128,1536]{1,0:T(8,128)(2,1)S(1)} %add_convert_fusion.3), channel_id=1, source_target_pairs={{0,24},{1,25},{2,26},{3,27},{4,28},{5,29},{6,30},{7,31},{8,16},{9,... | collective-permute-start | bytes 1179656 | tf_op jit(solution)/shard_map/ppermute | solution.py:40
  204.3 26.5 %collective-permute-start.26 = (bf16[128,1536]{1,0:T(8,128)(2,1)S(1)}, bf16[128,1536]{1,0:T(8,128)(2,1)S(1)}, u32[]{:S(2)}, u32[]{:S(2)}) collective-permute-start(bf16[128,1536]{1,0:T(8,128)(2,1)S(1)} %add_convert_fusion.1), channel_id=1, source_target_pairs={{0,16},{1,17},{2,18},{3,19},{4,20},{5,21},{6,22},{7,23},{8,24},{9,... | collective-permute-start | bytes 1179656 | tf_op jit(solution)/shard_map/ppermute | solution.py:40
  (34 other events, 391.4 us)
where the time goes:
time: 240 us; the launch traced here: 235 us
  waiting for transfers between devices  126 us (52%)
  starting transfers between devices  53.7 us (22%)
  Pallas kernels  31 us (13%)
  local copies, waits for them, and re-layouts  18.3 us (8%)
  other arithmetic  5.03 us (2%)
    ppermute x39, waiting for transfers between devices, move(): return lax.ppermute(block, ('section', 'ep'), pairs)  126 us
    ppermute x39, starting transfers between devices, move(): return lax.ppermute(block, ('section', 'ep'), pairs)  53.7 us
    unnamed x56, local copies, waits for them, and re-layouts  18.1 us
    pallas_call x4, Pallas kernels, weight_grads(): pl.pallas_call(functools.partial(weight_grads_kernel, n, cap, 2 * local,...  16 us
    pallas_call x1, Pallas kernels, token_grads(): pl.pallas_call(functools.partial(token_grads_kernel, n, cap, local), out_...  12.2 us
  transfers between devices with their start and end apart: 39, of which 18 were waited for; matrix products, arithmetic and copies ran while one was open for 3% of the time, Pallas kernels for 12%

commit v1 on v0

--- a/solution.py
+++ b/solution.py
@@ -123,7 +123,7 @@
         out_shape=outs,
         scratch_shapes=[pltpu.VMEM((n, groups * cap, width), BF16)],
         name="token_grads",
-        compiler_params=pltpu.CompilerParams(vmem_limit_bytes=36 << 20),
+        compiler_params=pltpu.CompilerParams(vmem_limit_bytes=26 << 20),
         cost_estimate=pl.CostEstimate(
             flops=4 * groups * n * cap * hidden * width, bytes_accessed=24 << 20, transcendentals=0
         ),
@@ -131,62 +131,82 @@
     return result[:n], result[n], result[n + 1]
 
 
-def weight_grads_kernel(n, cap, groups, group, added, *refs):
-    a_refs, x_refs = refs[:n], refs[n:2 * n]
-    up_ref, grad_rows_ref, cot_ref = refs[2 * n:2 * n + 3]
-    more = refs[2 * n + 3:2 * n + 3 + 2 * added]
-    grad_up_ref, grad_down_ref, x_ref = refs[-3:]
+def gather_kernel(n, cap, groups, *refs):
+    a_refs, x_refs, out_ref = refs[:n], refs[n:2 * n], refs[2 * n]
     tokens = x_refs[0].shape[0]
     for k in range(n):
-        pick = selection(a_refs[k], groups * cap, tokens, group * cap, cap)
-        x_ref[k * cap:(k + 1) * cap, :] = dot(pick, x_refs[k][...], TN).astype(BF16)
-    act = jnp.concatenate([a_refs[k][group * cap:(group + 1) * cap, :] for k in range(n)], axis=0)
-    hidden = (dot(x_ref[...], up_ref[0]) * act.astype(F32)).astype(BF16)
+        pick = selection(a_refs[k], groups * cap, tokens, 0, groups * cap)
+        rows = dot(pick, x_refs[k][...], TN).astype(BF16)
+        for g in range(groups):
+            out_ref[g, k * cap:(k + 1) * cap, :] = rows[g * cap:(g + 1) * cap]
+
+
+def gather(acts, xs, cap, groups):
+    n = len(acts)
+    width = xs[0].shape[1]
+    return pl.pallas_call(
+        functools.partial(gather_kernel, n, cap, groups),
+        out_shape=jax.ShapeDtypeStruct((groups, n * cap, width), BF16),
+        name="gather",
+        compiler_params=pltpu.CompilerParams(vmem_limit_bytes=20 << 20),
+        cost_estimate=pl.CostEstimate(
+            flops=2 * n * groups * cap * width * xs[0].shape[0], bytes_accessed=4 << 20, transcendentals=0
+        ),
+    )(*acts, *xs)
+
+
+def weight_grads_kernel(n, cap, first, added, *refs):
+    a_refs, (x_ref, up_ref, grad_rows_ref, cot_ref), more = refs[:n], refs[n:n + 4], refs[n + 4:n + 4 + 2 * added]
+    grad_up_ref, grad_down_ref = refs[-2:]
+    rows = pl.ds(pl.multiple_of((first + pl.program_id(0)) * cap, cap), cap)
+    act = jnp.concatenate([a_ref[rows, :] for a_ref in a_refs], axis=0)
+    hidden = (dot(x_ref[0], up_ref[0]) * act.astype(F32)).astype(BF16)
     grad_down = dot(hidden, cot_ref[0], TN)
-    grad_up = dot(x_ref[...], grad_rows_ref[0], TN)
-    if added:
-        grad_up = grad_up + more[0][0].astype(F32)
-        grad_down = grad_down + more[1][0].astype(F32)
+    grad_up = dot(x_ref[0], grad_rows_ref[0], TN)
+    for i in range(added):
+        grad_up = grad_up + more[2 * i][0].astype(F32)
+        grad_down = grad_down + more[2 * i + 1][0].astype(F32)
     grad_down_ref[0] = grad_down.astype(BF16)
     grad_up_ref[0] = grad_up.astype(BF16)
 
 
-def weight_grads(acts, xs, up, grad_rows, cot_rows, cap, group, more=(), total=1, into=()):
+def weight_grads(acts, x_rows, up, grad_rows, cot_rows, cap, group, count, more=(), total=None, into=()):
     n = len(acts)
     local, width, hidden = up.shape
-    rows = n * cap
-    mine = group if total > 1 else 0
+    at = 0 if total is None else group % local
+    total = count if total is None else total
 
     def whole(v):
         return pl.BlockSpec(v.shape, lambda i: (0,) * v.ndim)
 
-    def one(v, j):
-        return pl.BlockSpec((1, *v.shape[1:]), lambda i: (j, 0, 0))
+    def from_(v, j):
+        return pl.BlockSpec((1, *v.shape[1:]), lambda i: (j + i, 0, 0))
 
     outs = [
         jax.ShapeDtypeStruct((total, width, hidden), BF16),
         jax.ShapeDtypeStruct((total, hidden, width), BF16),
     ]
-    operands = (*acts, *xs, up, grad_rows, cot_rows, *more, *into)
-    first = len(operands) - len(into)
+    added = [(v, j) for pair, j in more for v in pair]
+    operands = (*acts, x_rows, up, grad_rows, cot_rows, *[v for v, _ in added], *into)
+    before = len(operands) - len(into)
     return pl.pallas_call(
-        functools.partial(weight_grads_kernel, n, cap, 2 * local, group, len(more) // 2),
-        grid=(1,),
+        functools.partial(weight_grads_kernel, n, cap, group, len(more)),
+        grid=(count,),
         in_specs=[
-            *[whole(v) for v in (*acts, *xs)],
-            one(up, group % local),
-            one(grad_rows, group),
-            one(cot_rows, group),
-            *[whole(v) for v in more],
+            *[whole(v) for v in acts],
+            from_(x_rows, group),
+            from_(up, group % local),
+            from_(grad_rows, group),
+            from_(cot_rows, group),
+            *[from_(v, j) for v, j in added],
             *[pl.BlockSpec(memory_space=pl.ANY) for _ in into],
         ],
-        out_specs=[one(v, mine) for v in outs],
+        out_specs=[from_(v, at) for v in outs],
         out_shape=outs,
-        input_output_aliases={first + i: i for i in range(len(into))},
-        scratch_shapes=[pltpu.VMEM((rows, width), BF16)],
-        compiler_params=pltpu.CompilerParams(vmem_limit_bytes=32 << 20),
+        input_output_aliases={before + i: i for i in range(len(into))},
+        compiler_params=pltpu.CompilerParams(vmem_limit_bytes=20 << 20),
         cost_estimate=pl.CostEstimate(
-            flops=6 * rows * hidden * width, bytes_accessed=12 << 20, transcendentals=0
+            flops=6 * count * n * cap * hidden * width, bytes_accessed=count * (8 << 20), transcendentals=0
         ),
     )(*operands)
 
@@ -222,14 +242,16 @@
     def inward(z, x, core):
         return {0: (1, x, core), 3: (2, x, core)}.get(z)
 
-    def spread(block, far_block=None, side=False):
+    def spread(block, side=False):
         rows = [block] + [None] * (zs - 1)
         if quads:
             rows[1] = grid.move(block, along_z(1))
             near = grid.move(block, middle)
-            rows[2] = grid.move(block, along_z(2)) if far_block is None else far_block
-            far = grid.move(rows[2], outward)
-            rows[3] = jnp.where(inner, near, far)
+            on = grid.move(rows[1], middle)
+            out1 = grid.move(near, outward)
+            out2 = grid.move(on, outward)
+            rows[2] = jnp.where(inner, on, out1)
+            rows[3] = jnp.where(inner, near, out2)
         else:
             for d in range(1, zs):
                 rows[d] = grid.move(block, along_z(d))
@@ -244,7 +266,6 @@
         return blocks
 
     cotangent = grid.move(upstream[0], along_z(0), -1)
-    cot_far = grid.move(upstream[0], along_z(2), -1) if quads else None
     tokens_all = spread(inputs[0])
 
     scale = route_weights[0][:, :, None]
@@ -256,16 +277,24 @@
     for k in range(1, grid.chips):
         acts.append(grid.move(blocks[k], lambda z, x, core, k=k: (z ^ (k // xs), x ^ (k % xs), core)))
 
-    cots = spread(cotangent, cot_far, quads)
+    cots = spread(cotangent, quads)
     ups = (w_up[0], grid.move(w_up[0], across))
     downs = (w_down[0], grid.move(w_down[0], across))
-    parts, grad_rows, cot_rows = token_grads(acts, cots, ups, downs, cap, local)
+    groups = 2 * local
+    split = zs // 2 * xs
+    halves = (range(split), range(split, grid.chips))
+    parts, grad_rows, cot_rows = [None] * grid.chips, [], []
+    for members in halves:
+        some, rows, cot = token_grads([acts[k] for k in members], [cots[k] for k in members], ups, downs, cap, local)
+        grad_rows.append(rows)
+        cot_rows.append(cot)
+        for k, part in zip(members, some):
+            parts[k] = part
 
     def total(*values):
         return functools.reduce(jnp.add, [v.astype(F32) for v in values]).astype(BF16)
 
     rows = [None] * zs
-    parts = list(parts)
     if quads:
         rows[1] = parts[xs]
         for d in range(1, xs):
@@ -282,13 +311,24 @@
     last.append(grid.move(rows[0], along_z(0), -1))
     delivered = total(*last)[None]
 
+    x_rows = []
+    for members in halves:
+        x_rows.append(gather([acts[k] for k in members], [tokens_all[k] for k in members], cap, groups))
+    sides = []
+    for h, members in enumerate(halves):
+        sides.append(([acts[k] for k in members], x_rows[h]))
+    near_half = []
+    for p in range(2):
+        near_half.append(weight_grads(*sides[0], ups[p], grad_rows[0], cot_rows[0], cap, p * local, local))
+    far_half = (*sides[1],)
     given = []
     for j in range(local):
-        theirs = weight_grads(acts, tokens_all, ups[1], grad_rows, cot_rows, cap, local + j)
+        theirs = weight_grads(*far_half, ups[1], grad_rows[1], cot_rows[1], cap, local + j, 1, [(near_half[1], j)])
         given.append([grid.move(theirs[0], across), grid.move(theirs[1], across)])
     ours = ()
     for j in range(local):
-        ours = weight_grads(acts, tokens_all, ups[0], grad_rows, cot_rows, cap, j, given[j], local, ours)
+        more = [(near_half[0], j), (given[j], 0)]
+        ours = weight_grads(*far_half, ups[0], grad_rows[1], cot_rows[1], cap, j, 1, more, local, ours)
     grad_up, grad_down = ours
     return (delivered, grad_up[None], grad_down[None])
 

time: 240 us -> 230 us (0.958)
  local copies, waits for them, and re-layouts: 18.3 us -> 1.11 us
  Pallas kernels: 31 us -> 37.9 us
    unnamed x56 -> x14, local copies, waits for them, and re-layouts: 18.1 us -> 0.92 us
    pallas_call x1 -> x2, Pallas kernels: 12.2 us -> 15.9 us  [token_grads(): pl.pallas_call(functools.partial(token_grads_kernel, n, cap, local), out_...]
    pallas_call x4 -> x8, Pallas kernels: 16 us -> 19.1 us  [the longest x6 16.6 us: weight_grads(): pl.pallas_call(functools.partial(weight_grads_kernel, n, cap, group, len(...]
    ppermute x39 -> x41, waiting for transfers between devices: 126 us -> 127 us  [move(): return lax.ppermute(block, ('section', 'ep'), pairs)]
    ppermute x39 -> x41, starting transfers between devices: 53.7 us -> 53.1 us  [move(): return lax.ppermute(block, ('section', 'ep'), pairs)]
  transfers between devices with their start and end apart: 39 -> 41, of which waited for: 18 -> 18; matrix products, arithmetic and copies ran while one was open for 3% -> 3% of each run, Pallas kernels for 12% -> 16%
where the time goes in v1:
time: 230 us; the launch traced here: 226 us
  waiting for transfers between devices  127 us (55%)
  starting transfers between devices  53.1 us (23%)
  Pallas kernels  37.9 us (16%)
  other arithmetic  6.19 us (3%)
    ppermute x41, waiting for transfers between devices, move(): return lax.ppermute(block, ('section', 'ep'), pairs)  127 us
    ppermute x41, starting transfers between devices, move(): return lax.ppermute(block, ('section', 'ep'), pairs)  53.1 us
    pallas_call x6, Pallas kernels, weight_grads(): pl.pallas_call(functools.partial(weight_grads_kernel, n, cap, group, len(...  16.6 us
    pallas_call x2, Pallas kernels, token_grads(): pl.pallas_call(functools.partial(token_grads_kernel, n, cap, local), out_...  15.9 us
  transfers between devices with their start and end apart: 41, of which 18 were waited for; matrix products, arithmetic and copies ran while one was open for 3% of the time, Pallas kernels for 16%

profile of v1, /device:TPU:10, one launch (start us, length us, event | category | flops | bytes accessed | tf_op | source)
XLA Modules:
  0.0 226.3 jit_solution(7436449332124811594)
XLA Ops:
  1.2 4.6 %collective-permute-start.30 = (bf16[128,1536]{1,0:T(8,128)(2,1)}, bf16[128,1536]{1,0:T(8,128)(2,1)}, u32[]{:S(2)}, u32[]{:S(2)}) collective-permute-start(bf16[128,1536]{1,0:T(8,128)(2,1)} %bitcast.18), channel_id=1, source_target_pairs={{4,8},{5,9},{6,10},{7,11},{8,4},{9,5},{10,6},{11,7},{20,24},{21,25... | collective-permute-start | bytes 1179656 | tf_op jit(solution)/shard_map/ppermute | solution.py:40
  10.0 2.8 %prep.1 = (bf16[200,384]{1,0:T(8,128)(2,1)S(1)}, bf16[200,384]{1,0:T(8,128)(2,1)S(1)}, bf16[200,384]{1,0:T(8,128)(2,1)S(1)}, bf16[200,384]{1,0:T(8,128)(2,1)S(1)...) custom-call(s32[1,1024]{1,0:T(1,128)S(1)} %reshape_squeeze.3.ids_ref, ...), custom_call_target="tpu_custom_call" | custom-call | flops 1610612736 | bytes 1572864 | tf_op jit(solution)/shard_map/prep/pallas_call | solution.py:70
  13.5 2.9 %collective-permute-done.4.refs_4_ = bf16[128,1536]{1,0:T(8,128)(2,1)} collective-permute-done((bf16[128,1536]{1,0:T(8,128)(2,1)}, bf16[128,1536]{1,0:T(8,128)(2,1)}, u32[]{:S(2)}, u32[]{:S(2)}) %collective-permute-start.4) | collective-permute-done | bytes 393248 | tf_op jit(solution)/shard_map/ppermute | solution.py:40
  20.1 3.9 %collective-permute-start.29 = (bf16[128,1536]{1,0:T(8,128)(2,1)}, bf16[128,1536]{1,0:T(8,128)(2,1)}, u32[]{:S(2)}, u32[]{:S(2)}) collective-permute-start(bf16[128,1536]{1,0:T(8,128)(2,1)} %collective-permute-done.28.refs_6_), channel_id=1, source_target_pairs={{4,8},{5,9},{6,10},{7,11},{8,4},{9,5},{10,6},{11,7},{20,24},{21,25... | collective-permute-start | bytes 1179656 | tf_op jit(solution)/shard_map/ppermute | solution.py:40
  26.1 10.3 %collective-permute-done.21.refs_3_ = bf16[200,384]{1,0:T(8,128)(2,1)S(1)} collective-permute-done((bf16[200,384]{1,0:T(8,128)(2,1)S(1)}, bf16[200,384]{1,0:T(8,128)(2,1)S(1)}, u32[]{:S(2)}, u32[]{:S(2)}) %collective-permute-start.21) | collective-permute-done | bytes 153632 | tf_op jit(solution)/shard_map/ppermute | solution.py:40
  36.4 2.9 %collective-permute-start = (bf16[200,384]{1,0:T(8,128)(2,1)S(1)}, bf16[200,384]{1,0:T(8,128)(2,1)S(1)}, u32[]{:S(2)}, u32[]{:S(2)}) collective-permute-start(bf16[200,384]{1,0:T(8,128)(2,1)S(1)} %get-tuple-element.35), channel_id=1, source_target_pairs={{0,8},{1,9},{2,10},{3,11},{4,12},{5,13},{6,14},{7,15},{8,0},{9,1},... | collective-permute-start | bytes 460808 | tf_op jit(solution)/shard_map/ppermute | solution.py:40
  39.3 4.9 %collective-permute-done.refs_0_ = bf16[200,384]{1,0:T(8,128)(2,1)S(1)} collective-permute-done((bf16[200,384]{1,0:T(8,128)(2,1)S(1)}, bf16[200,384]{1,0:T(8,128)(2,1)S(1)}, u32[]{:S(2)}, u32[]{:S(2)}) %collective-permute-start) | collective-permute-done | bytes 153632 | tf_op jit(solution)/shard_map/ppermute | solution.py:40
  44.8 3.0 %collective-permute-start.1 = (bf16[200,384]{1,0:T(8,128)(2,1)}, bf16[200,384]{1,0:T(8,128)(2,1)S(1)}, u32[]{:S(2)}, u32[]{:S(2)}) collective-permute-start(bf16[200,384]{1,0:T(8,128)(2,1)} %copy-done.4), channel_id=1, source_target_pairs={{0,10},{1,11},{2,8},{3,9},{4,14},{5,15},{6,12},{7,13},{8,2},{9,3},... | collective-permute-start | bytes 460808 | tf_op jit(solution)/shard_map/ppermute | solution.py:40
  47.8 3.3 %collective-permute-start.6 = (bf16[128,1536]{1,0:T(8,128)(2,1)S(1)}, bf16[128,1536]{1,0:T(8,128)(2,1)S(1)}, u32[]{:S(2)}, u32[]{:S(2)}) collective-permute-start(bf16[128,1536]{1,0:T(8,128)(2,1)S(1)} %collective-permute-done.5.refs_6_), channel_id=1, source_target_pairs={{4,8},{5,9},{6,10},{7,11},{8,4},{9,5},{10,6},{11,7},{20,24},{21,25... | collective-permute-start | bytes 1179656 | tf_op jit(solution)/shard_map/ppermute | solution.py:40
  55.7 15.4 %collective-permute-done.6 = bf16[128,1536]{1,0:T(8,128)(2,1)S(1)} collective-permute-done((bf16[128,1536]{1,0:T(8,128)(2,1)S(1)}, bf16[128,1536]{1,0:T(8,128)(2,1)S(1)}, u32[]{:S(2)}, u32[]{:S(2)}) %collective-permute-start.6) | collective-permute-done | bytes 393248 | tf_op jit(solution)/shard_map/ppermute | solution.py:40
  75.2 2.9 %collective-permute-done.3.refs_3_ = bf16[200,384]{1,0:T(8,128)(2,1)S(1)} collective-permute-done((bf16[200,384]{1,0:T(8,128)(2,1)}, bf16[200,384]{1,0:T(8,128)(2,1)S(1)}, u32[]{:S(2)}, u32[]{:S(2)}) %collective-permute-start.3) | collective-permute-done | bytes 153632 | tf_op jit(solution)/shard_map/ppermute | solution.py:40
  79.2 4.0 %collective-permute-done.33 = bf16[128,1536]{1,0:T(8,128)(2,1)S(1)} collective-permute-done((bf16[128,1536]{1,0:T(8,128)(2,1)}, bf16[128,1536]{1,0:T(8,128)(2,1)S(1)}, u32[]{:S(2)}, u32[]{:S(2)}) %collective-permute-start.33) | collective-permute-done | bytes 393248 | tf_op jit(solution)/shard_map/ppermute | solution.py:40
  83.2 4.5 %collective-permute-start.10 = (bf16[128,1536]{1,0:T(8,128)(2,1)S(1)}, bf16[128,1536]{1,0:T(8,128)(2,1)S(1)}, u32[]{:S(2)}, u32[]{:S(2)}) collective-permute-start(bf16[128,1536]{1,0:T(8,128)(2,1)S(1)} %collective-permute-done.6), channel_id=1, source_target_pairs={{4,0},{5,1},{6,2},{7,3},{8,12},{9,13},{10,14},{11,15},{20,16},{21,... | collective-permute-start | bytes 1179656 | tf_op jit(solution)/shard_map/ppermute | solution.py:40
  89.5 5.5 %collective-permute-done.22.refs_5_ = bf16[128,1536]{1,0:T(8,128)(2,1)S(1)} collective-permute-done((bf16[128,1536]{1,0:T(8,128)(2,1)}, bf16[128,1536]{1,0:T(8,128)(2,1)S(1)}, u32[]{:S(2)}, u32[]{:S(2)}) %collective-permute-start.22) | collective-permute-done | bytes 393248 | tf_op jit(solution)/shard_map/ppermute | solution.py:40
  98.1 5.4 %collective-permute-done.36.refs_7_ = bf16[128,1536]{1,0:T(8,128)(2,1)S(1)} collective-permute-done((bf16[128,1536]{1,0:T(8,128)(2,1)}, bf16[128,1536]{1,0:T(8,128)(2,1)S(1)}, u32[]{:S(2)}, u32[]{:S(2)}) %collective-permute-start.36) | collective-permute-done | bytes 393248 | tf_op jit(solution)/shard_map/ppermute | solution.py:40
  104.4 7.4 %collective-permute-done.32.refs_5_ = bf16[128,1536]{1,0:T(8,128)(2,1)S(1)} collective-permute-done((bf16[128,1536]{1,0:T(8,128)(2,1)S(1)}, bf16[128,1536]{1,0:T(8,128)(2,1)S(1)}, u32[]{:S(2)}, u32[]{:S(2)}) %collective-permute-start.32) | collective-permute-done | bytes 393248 | tf_op jit(solution)/shard_map/ppermute | solution.py:40
  112.9 7.4 %collective-permute-done.34.refs_7_ = bf16[128,1536]{1,0:T(8,128)(2,1)S(1)} collective-permute-done((bf16[128,1536]{1,0:T(8,128)(2,1)S(1)}, bf16[128,1536]{1,0:T(8,128)(2,1)S(1)}, u32[]{:S(2)}, u32[]{:S(2)}) %collective-permute-start.34) | collective-permute-done | bytes 393248 | tf_op jit(solution)/shard_map/ppermute | solution.py:40
  122.9 5.8 %collective-permute-done.9.refs_5_ = bf16[128,1536]{1,0:T(8,128)(2,1)S(1)} collective-permute-done((bf16[128,1536]{1,0:T(8,128)(2,1)S(1)}, bf16[128,1536]{1,0:T(8,128)(2,1)S(1)}, u32[]{:S(2)}, u32[]{:S(2)}) %collective-permute-start.9) | collective-permute-done | bytes 393248 | tf_op jit(solution)/shard_map/ppermute | solution.py:40
  128.7 8.3 %collective-permute-done.11.refs_7_ = bf16[128,1536]{1,0:T(8,128)(2,1)S(1)} collective-permute-done((bf16[128,1536]{1,0:T(8,128)(2,1)S(1)}, bf16[128,1536]{1,0:T(8,128)(2,1)S(1)}, u32[]{:S(2)}, u32[]{:S(2)}) %collective-permute-start.11) | collective-permute-done | bytes 393248 | tf_op jit(solution)/shard_map/ppermute | solution.py:40
  137.0 7.9 %token_grads.2 = (bf16[128,1536]{1,0:T(8,128)(2,1)S(1)}, bf16[128,1536]{1,0:T(8,128)(2,1)S(1)}, bf16[128,1536]{1,0:T(8,128)(2,1)S(1)}, bf16[128,1536]{1,0:T(8,12...) custom-call(bf16[200,384]{1,0:T(8,128)(2,1)S(1)} %collective-permute-done.refs_0_, ...), custom_call_target="tpu_custom_call" | custom-call | flops 1811939328 | bytes 25165824 | tf_op jit(solution)/shard_map/token_grads/pallas_call | solution.py:121
  146.0 8.0 %token_grads.3 = (bf16[128,1536]{1,0:T(8,128)(2,1)S(1)}, bf16[128,1536]{1,0:T(8,128)(2,1)S(1)}, bf16[128,1536]{1,0:T(8,128)(2,1)S(1)}, bf16[128,1536]{1,0:T(8,12...) custom-call(bf16[200,384]{1,0:T(8,128)(2,1)S(1)} %get-tuple-element.43.refs_0_, ...), custom_call_target="tpu_custom_call" | custom-call | flops 1811939328 | bytes 25165824 | tf_op jit(solution)/shard_map/token_grads/pallas_call | solution.py:121
  156.9 4.1 %shard_map.95 = (bf16[2,1536,384]{2,1,0:T(8,128)(2,1)S(1)}, bf16[2,384,1536]{2,1,0:T(8,128)(2,1)S(1)}) custom-call(bf16[200,384]{1,0:T(8,128)(2,1)S(1)} %get-tuple-element.43.refs_0_, bf16[200,384]{1,0:T(8,128)(2,1)S(1)} %collective-permute-done.19.refs_1_, bf16[200,384]{1,0:T(8,128)(2,1)S(1)} %collective-permute-done.20.refs_2_, ...), custom_call_target="tpu_custom_call" | custom-call | flops 1358954496 | bytes 16777216 | tf_op jit(solution)/shard_map/pallas_call | solution.py:192
  161.0 2.5 %shard_map.97 = (bf16[1,1536,384]{2,1,0:T(8,128)(2,1)S(1)}, bf16[1,384,1536]{2,1,0:T(8,128)(2,1)S(1)}) custom-call(bf16[200,384]{1,0:T(8,128)(2,1)S(1)} %collective-permute-done.refs_0_, bf16[200,384]{1,0:T(8,128)(2,1)S(1)} %collective-permute-done.1.refs_1_, bf16[200,384]{1,0:T(8,128)(2,1)S(1)} %collective-permute-done.2.refs_2_, ...), custom_call_target="tpu_custom_call" | custom-call | flops 679477248 | bytes 8388608 | tf_op jit(solution)/shard_map/pallas_call | solution.py:192
  163.6 2.5 %shard_map.96 = (bf16[1,1536,384]{2,1,0:T(8,128)(2,1)S(1)}, bf16[1,384,1536]{2,1,0:T(8,128)(2,1)S(1)}) custom-call(bf16[200,384]{1,0:T(8,128)(2,1)S(1)} %collective-permute-done.refs_0_, bf16[200,384]{1,0:T(8,128)(2,1)S(1)} %collective-permute-done.1.refs_1_, bf16[200,384]{1,0:T(8,128)(2,1)S(1)} %collective-permute-done.2.refs_2_, ...), custom_call_target="tpu_custom_call" | custom-call | flops 679477248 | bytes 8388608 | tf_op jit(solution)/shard_map/pallas_call | solution.py:192
  168.2 13.5 %collective-permute-done.17 = bf16[128,1536]{1,0:T(8,128)(2,1)S(1)} collective-permute-done((bf16[128,1536]{1,0:T(8,128)(2,1)S(1)}, bf16[128,1536]{1,0:T(8,128)(2,1)S(1)}, u32[]{:S(2)}, u32[]{:S(2)}) %collective-permute-start.17) | collective-permute-done | bytes 393248 | tf_op jit(solution)/shard_map/ppermute | solution.py:40
  182.8 8.8 %collective-permute-done.26 = bf16[128,1536]{1,0:T(8,128)(2,1)S(1)} collective-permute-done((bf16[128,1536]{1,0:T(8,128)(2,1)S(1)}, bf16[128,1536]{1,0:T(8,128)(2,1)S(1)}, u32[]{:S(2)}, u32[]{:S(2)}) %collective-permute-start.26) | collective-permute-done | bytes 393248 | tf_op jit(solution)/shard_map/ppermute | solution.py:40
  191.8 3.1 %collective-permute-start.15 = (bf16[128,1536]{1,0:T(8,128)(2,1)S(1)}, bf16[128,1536]{1,0:T(8,128)(2,1)S(1)}, u32[]{:S(2)}, u32[]{:S(2)}) collective-permute-start(bf16[128,1536]{1,0:T(8,128)(2,1)S(1)} %add_convert_fusion.5), channel_id=1, source_target_pairs={{4,24},{5,25},{6,26},{7,27},{8,20},{9,21},{10,22},{11,23},{20,8},{... | collective-permute-start | bytes 1179656 | tf_op jit(solution)/shard_map/ppermute | solution.py:40
  196.2 2.8 %shard_map.94 = (bf16[2,1536,384]{2,1,0:T(8,128)(2,1)S(1)}, bf16[2,384,1536]{2,1,0:T(8,128)(2,1)S(1)}) custom-call(bf16[200,384]{1,0:T(8,128)(2,1)S(1)} %get-tuple-element.43.refs_0_, bf16[200,384]{1,0:T(8,128)(2,1)S(1)} %collective-permute-done.19.refs_1_, bf16[200,384]{1,0:T(8,128)(2,1)S(1)} %collective-permute-done.20.refs_2_, ...), custom_call_target="tpu_custom_call" | custom-call | flops 1358954496 | bytes 16777216 | tf_op jit(solution)/shard_map/pallas_call | solution.py:192
  199.0 2.4 %shard_map.98 = (bf16[2,1536,384]{2,1,0:T(8,128)(2,1)}, bf16[2,384,1536]{2,1,0:T(8,128)(2,1)}) custom-call(bf16[200,384]{1,0:T(8,128)(2,1)S(1)} %collective-permute-done.refs_0_, bf16[200,384]{1,0:T(8,128)(2,1)S(1)} %collective-permute-done.1.refs_1_, bf16[200,384]{1,0:T(8,128)(2,1)S(1)} %collective-permute-done.2.refs_2_, ...), custom_call_target="tpu_custom_call" | custom-call | flops 679477248 | bytes 8388608 | tf_op jit(solution)/shard_map/pallas_call | solution.py:192
  201.4 13.7 %collective-permute-done.15 = bf16[128,1536]{1,0:T(8,128)(2,1)S(1)} collective-permute-done((bf16[128,1536]{1,0:T(8,128)(2,1)S(1)}, bf16[128,1536]{1,0:T(8,128)(2,1)S(1)}, u32[]{:S(2)}, u32[]{:S(2)}) %collective-permute-start.15) | collective-permute-done | bytes 393248 | tf_op jit(solution)/shard_map/ppermute | solution.py:40
  215.0 7.9 %collective-permute-done.27 = bf16[128,1536]{1,0:T(8,128)(2,1)S(1)} collective-permute-done((bf16[128,1536]{1,0:T(8,128)(2,1)S(1)}, bf16[128,1536]{1,0:T(8,128)(2,1)S(1)}, u32[]{:S(2)}, u32[]{:S(2)}) %collective-permute-start.27) | collective-permute-done | bytes 393248 | tf_op jit(solution)/shard_map/ppermute | solution.py:40
  223.9 2.4 %shard_map.99 = (bf16[2,1536,384]{2,1,0:T(8,128)(2,1)}, bf16[2,384,1536]{2,1,0:T(8,128)(2,1)}) custom-call(bf16[200,384]{1,0:T(8,128)(2,1)S(1)} %collective-permute-done.refs_0_, bf16[200,384]{1,0:T(8,128)(2,1)S(1)} %collective-permute-done.1.refs_1_, ...), custom_call_target="tpu_custom_call", output_to_operand_aliasing={{0}: (12, {}), {1}: (13, {})} | custom-call | flops 679477248 | bytes 8388608 | tf_op jit(solution)/shard_map/pallas_call | solution.py:192
  (87 shorter events, 40.6 us)
Async XLA Ops:
  0.6 19.5 %collective-permute-start.28 = (bf16[128,1536]{1,0:T(8,128)(2,1)}, bf16[128,1536]{1,0:T(8,128)(2,1)}, u32[]{:S(2)}, u32[]{:S(2)}) collective-permute-start(bf16[128,1536]{1,0:T(8,128)(2,1)} %bitcast.17), channel_id=1, source_target_pairs={{0,4},{1,5},{2,6},{3,7},{4,0},{5,1},{6,2},{7,3},{8,12},{9,13},{10,... | collective-permute-start | bytes 1179656 | tf_op jit(solution)/shard_map/ppermute | solution.py:40
  1.2 22.9 %collective-permute-start.30 = (bf16[128,1536]{1,0:T(8,128)(2,1)}, bf16[128,1536]{1,0:T(8,128)(2,1)}, u32[]{:S(2)}, u32[]{:S(2)}) collective-permute-start(bf16[128,1536]{1,0:T(8,128)(2,1)} %bitcast.18), channel_id=1, source_target_pairs={{4,8},{5,9},{6,10},{7,11},{8,4},{9,5},{10,6},{11,7},{20,24},{21,25... | collective-permute-start | bytes 1179656 | tf_op jit(solution)/shard_map/ppermute | solution.py:40
  13.5 12.6 %collective-permute-start.20 = (bf16[200,384]{1,0:T(8,128)(2,1)S(1)}, bf16[200,384]{1,0:T(8,128)(2,1)S(1)}, u32[]{:S(2)}, u32[]{:S(2)}) collective-permute-start(bf16[200,384]{1,0:T(8,128)(2,1)S(1)} %get-tuple-element.45), channel_id=1, source_target_pairs={{0,4},{1,5},{2,6},{3,7},{4,0},{5,1},{6,2},{7,3},{8,12},{9,13},{10,... | collective-permute-start | bytes 460808 | tf_op jit(solution)/shard_map/ppermute | solution.py:40
  16.4 27.8 %collective-permute-start.5 = (bf16[128,1536]{1,0:T(8,128)(2,1)}, bf16[128,1536]{1,0:T(8,128)(2,1)S(1)}, u32[]{:S(2)}, u32[]{:S(2)}) collective-permute-start(bf16[128,1536]{1,0:T(8,128)(2,1)} %collective-permute-done.4.refs_4_), channel_id=1, source_target_pairs={{0,4},{1,5},{2,6},{3,7},{4,0},{5,1},{6,2},{7,3},{8,12},{9,13},{10,... | collective-permute-start | bytes 1179656 | tf_op jit(solution)/shard_map/ppermute | solution.py:40
  18.2 26.6 %collective-permute-start.7 = (bf16[128,1536]{1,0:T(8,128)(2,1)}, bf16[128,1536]{1,0:T(8,128)(2,1)}, u32[]{:S(2)}, u32[]{:S(2)}) collective-permute-start(bf16[128,1536]{1,0:T(8,128)(2,1)} %collective-permute-done.4.refs_4_), channel_id=1, source_target_pairs={{4,8},{5,9},{6,10},{7,11},{8,4},{9,5},{10,6},{11,7},{20,24},{21,25... | collective-permute-start | bytes 1179656 | tf_op jit(solution)/shard_map/ppermute | solution.py:40
  20.1 27.7 %collective-permute-start.29 = (bf16[128,1536]{1,0:T(8,128)(2,1)}, bf16[128,1536]{1,0:T(8,128)(2,1)}, u32[]{:S(2)}, u32[]{:S(2)}) collective-permute-start(bf16[128,1536]{1,0:T(8,128)(2,1)} %collective-permute-done.28.refs_6_), channel_id=1, source_target_pairs={{4,8},{5,9},{6,10},{7,11},{8,4},{9,5},{10,6},{11,7},{20,24},{21,25... | collective-permute-start | bytes 1179656 | tf_op jit(solution)/shard_map/ppermute | solution.py:40
  24.1 27.1 %collective-permute-start.31 = (bf16[128,1536]{1,0:T(8,128)(2,1)}, bf16[128,1536]{1,0:T(8,128)(2,1)}, u32[]{:S(2)}, u32[]{:S(2)}) collective-permute-start(bf16[128,1536]{1,0:T(8,128)(2,1)} %collective-permute-done.30), channel_id=1, source_target_pairs={{4,0},{5,1},{6,2},{7,3},{8,12},{9,13},{10,14},{11,15},{20,16},{21,... | collective-permute-start | bytes 1179656 | tf_op jit(solution)/shard_map/ppermute | solution.py:40
  44.2 92.8 %collective-permute-start.12 = (bf16[2,1536,384]{2,1,0:T(8,128)(2,1)S(1)}, bf16[2,1536,384]{2,1,0:T(8,128)(2,1)}, u32[]{:S(2)}, u32[]{:S(2)}) collective-permute-start(bf16[2,1536,384]{2,1,0:T(8,128)(2,1)S(1)} %bitcast.11), channel_id=1, source_target_pairs={{0,1},{1,0},{2,3},{3,2},{4,5},{5,4},{6,7},{7,6},{8,9},{9,8},{10,11... | collective-permute-start | bytes 7077896 | tf_op jit(solution)/shard_map/ppermute | solution.py:40
  44.2 92.8 %collective-permute-start.13 = (bf16[2,384,1536]{2,1,0:T(8,128)(2,1)}, bf16[2,384,1536]{2,1,0:T(8,128)(2,1)}, u32[]{:S(2)}, u32[]{:S(2)}) collective-permute-start(bf16[2,384,1536]{2,1,0:T(8,128)(2,1)} %bitcast.4.refs_10_), channel_id=1, source_target_pairs={{0,1},{1,0},{2,3},{3,2},{4,5},{5,4},{6,7},{7,6},{8,9},{9,8},{10,11... | collective-permute-start | bytes 7077896 | tf_op jit(solution)/shard_map/ppermute | solution.py:40
  47.8 23.3 %collective-permute-start.6 = (bf16[128,1536]{1,0:T(8,128)(2,1)S(1)}, bf16[128,1536]{1,0:T(8,128)(2,1)S(1)}, u32[]{:S(2)}, u32[]{:S(2)}) collective-permute-start(bf16[128,1536]{1,0:T(8,128)(2,1)S(1)} %collective-permute-done.5.refs_6_), channel_id=1, source_target_pairs={{4,8},{5,9},{6,10},{7,11},{8,4},{9,5},{10,6},{11,7},{20,24},{21,25... | collective-permute-start | bytes 1179656 | tf_op jit(solution)/shard_map/ppermute | solution.py:40
  51.2 21.0 %collective-permute-start.8 = (bf16[128,1536]{1,0:T(8,128)(2,1)}, bf16[128,1536]{1,0:T(8,128)(2,1)S(1)}, u32[]{:S(2)}, u32[]{:S(2)}) collective-permute-start(bf16[128,1536]{1,0:T(8,128)(2,1)} %collective-permute-done.7), channel_id=1, source_target_pairs={{4,0},{5,1},{6,2},{7,3},{8,12},{9,13},{10,14},{11,15},{20,16},{21,... | collective-permute-start | bytes 1179656 | tf_op jit(solution)/shard_map/ppermute | solution.py:40
  54.7 19.7 %collective-permute-start.2 = (bf16[200,384]{1,0:T(8,128)(2,1)}, bf16[200,384]{1,0:T(8,128)(2,1)S(1)}, u32[]{:S(2)}, u32[]{:S(2)}) collective-permute-start(bf16[200,384]{1,0:T(8,128)(2,1)} %copy-done.3), channel_id=1, source_target_pairs={{0,12},{1,13},{2,14},{3,15},{4,8},{5,9},{6,10},{7,11},{8,4},{9,5},... | collective-permute-start | bytes 460808 | tf_op jit(solution)/shard_map/ppermute | solution.py:40
  74.4 14.3 %collective-permute-start.35 = (bf16[128,1536]{1,0:T(8,128)(2,1)S(1)}, bf16[128,1536]{1,0:T(8,128)(2,1)S(1)}, u32[]{:S(2)}, u32[]{:S(2)}) collective-permute-start(bf16[128,1536]{1,0:T(8,128)(2,1)S(1)} %bitcast.19), channel_id=1, source_target_pairs={{0,2},{1,3},{2,0},{3,1},{4,6},{5,7},{6,4},{7,5},{8,10},{9,11},{10,... | collective-permute-start | bytes 1179656 | tf_op jit(solution)/shard_map/ppermute | solution.py:40
  78.1 16.8 %collective-permute-start.22 = (bf16[128,1536]{1,0:T(8,128)(2,1)}, bf16[128,1536]{1,0:T(8,128)(2,1)S(1)}, u32[]{:S(2)}, u32[]{:S(2)}) collective-permute-start(bf16[128,1536]{1,0:T(8,128)(2,1)} %collective-permute-done.4.refs_4_), channel_id=1, source_target_pairs={{0,2},{1,3},{2,0},{3,1},{4,6},{5,7},{6,4},{7,5},{8,10},{9,11},{10,... | collective-permute-start | bytes 1179656 | tf_op jit(solution)/shard_map/ppermute | solution.py:40
  83.2 12.8 %collective-permute-start.10 = (bf16[128,1536]{1,0:T(8,128)(2,1)S(1)}, bf16[128,1536]{1,0:T(8,128)(2,1)S(1)}, u32[]{:S(2)}, u32[]{:S(2)}) collective-permute-start(bf16[128,1536]{1,0:T(8,128)(2,1)S(1)} %collective-permute-done.6), channel_id=1, source_target_pairs={{4,0},{5,1},{6,2},{7,3},{8,12},{9,13},{10,14},{11,15},{20,16},{21,... | collective-permute-start | bytes 1179656 | tf_op jit(solution)/shard_map/ppermute | solution.py:40
  88.7 14.7 %collective-permute-start.36 = (bf16[128,1536]{1,0:T(8,128)(2,1)}, bf16[128,1536]{1,0:T(8,128)(2,1)S(1)}, u32[]{:S(2)}, u32[]{:S(2)}) collective-permute-start(bf16[128,1536]{1,0:T(8,128)(2,1)} %collective-permute-done.28.refs_6_), channel_id=1, source_target_pairs={{0,2},{1,3},{2,0},{3,1},{4,6},{5,7},{6,4},{7,5},{8,10},{9,11},{10,... | collective-permute-start | bytes 1179656 | tf_op jit(solution)/shard_map/ppermute | solution.py:40
  95.0 16.9 %collective-permute-start.32 = (bf16[128,1536]{1,0:T(8,128)(2,1)S(1)}, bf16[128,1536]{1,0:T(8,128)(2,1)S(1)}, u32[]{:S(2)}, u32[]{:S(2)}) collective-permute-start(bf16[128,1536]{1,0:T(8,128)(2,1)S(1)} %broadcast_select_fusion.1.refs_4_), channel_id=1, source_target_pairs={{0,2},{1,3},{2,0},{3,1},{4,6},{5,7},{6,4},{7,5},{8,10},{9,11},{10,... | collective-permute-start | bytes 1179656 | tf_op jit(solution)/shard_map/ppermute | solution.py:40
  96.0 24.3 %collective-permute-start.34 = (bf16[128,1536]{1,0:T(8,128)(2,1)S(1)}, bf16[128,1536]{1,0:T(8,128)(2,1)S(1)}, u32[]{:S(2)}, u32[]{:S(2)}) collective-permute-start(bf16[128,1536]{1,0:T(8,128)(2,1)S(1)} %broadcast_select_fusion.refs_6_), channel_id=1, source_target_pairs={{0,2},{1,3},{2,0},{3,1},{4,6},{5,7},{6,4},{7,5},{8,10},{9,11},{10,... | collective-permute-start | bytes 1179656 | tf_op jit(solution)/shard_map/ppermute | solution.py:40
  103.4 25.3 %collective-permute-start.9 = (bf16[128,1536]{1,0:T(8,128)(2,1)S(1)}, bf16[128,1536]{1,0:T(8,128)(2,1)S(1)}, u32[]{:S(2)}, u32[]{:S(2)}) collective-permute-start(bf16[128,1536]{1,0:T(8,128)(2,1)S(1)} %broadcast_select_fusion.3.refs_4_), channel_id=1, source_target_pairs={{0,2},{1,3},{2,0},{3,1},{4,6},{5,7},{6,4},{7,5},{8,10},{9,11},{10,... | collective-permute-start | bytes 1179656 | tf_op jit(solution)/shard_map/ppermute | solution.py:40
  111.8 25.2 %collective-permute-start.11 = (bf16[128,1536]{1,0:T(8,128)(2,1)S(1)}, bf16[128,1536]{1,0:T(8,128)(2,1)S(1)}, u32[]{:S(2)}, u32[]{:S(2)}) collective-permute-start(bf16[128,1536]{1,0:T(8,128)(2,1)S(1)} %broadcast_select_fusion.2.refs_6_), channel_id=1, source_target_pairs={{0,2},{1,3},{2,0},{3,1},{4,6},{5,7},{6,4},{7,5},{8,10},{9,11},{10,... | collective-permute-start | bytes 1179656 | tf_op jit(solution)/shard_map/ppermute | solution.py:40
  120.3 25.7 %collective-permute-start.23 = (bf16[128,1536]{1,0:T(8,128)(2,1)S(1)}, bf16[128,1536]{1,0:T(8,128)(2,1)S(1)}, u32[]{:S(2)}, u32[]{:S(2)}) collective-permute-start(bf16[128,1536]{1,0:T(8,128)(2,1)S(1)} %collective-permute-done.22.refs_5_), channel_id=1, source_target_pairs={{0,4},{1,5},{2,6},{3,7},{4,0},{5,1},{6,2},{7,3},{8,12},{9,13},{10,... | collective-permute-start | bytes 1179656 | tf_op jit(solution)/shard_map/ppermute | solution.py:40
  144.9 21.1 %collective-permute-start.14 = (bf16[128,1536]{1,0:T(8,128)(2,1)S(1)}, bf16[128,1536]{1,0:T(8,128)(2,1)S(1)}, u32[]{:S(2)}, u32[]{:S(2)}) collective-permute-start(bf16[128,1536]{1,0:T(8,128)(2,1)S(1)} %get-tuple-element.40), channel_id=1, source_target_pairs={{0,2},{1,3},{2,0},{3,1},{4,6},{5,7},{6,4},{7,5},{8,10},{9,11},{10,... | collective-permute-start | bytes 1179656 | tf_op jit(solution)/shard_map/ppermute | solution.py:40
  154.0 12.7 %collective-permute-start.25 = (bf16[128,1536]{1,0:T(8,128)(2,1)S(1)}, bf16[128,1536]{1,0:T(8,128)(2,1)S(1)}, u32[]{:S(2)}, u32[]{:S(2)}) collective-permute-start(bf16[128,1536]{1,0:T(8,128)(2,1)S(1)} %get-tuple-element.50), channel_id=1, source_target_pairs={{0,4},{1,5},{2,6},{3,7},{4,0},{5,1},{6,2},{7,3},{8,12},{9,13},{10,... | collective-permute-start | bytes 1179656 | tf_op jit(solution)/shard_map/ppermute | solution.py:40
  154.1 37.7 %collective-permute-start.24 = (bf16[128,1536]{1,0:T(8,128)(2,1)S(1)}, bf16[128,1536]{1,0:T(8,128)(2,1)S(1)}, u32[]{:S(2)}, u32[]{:S(2)}) collective-permute-start(bf16[128,1536]{1,0:T(8,128)(2,1)S(1)} %get-tuple-element.47), channel_id=1, source_target_pairs={{0,20},{1,21},{2,22},{3,23},{4,16},{5,17},{6,18},{7,19},{8,28},{9,... | collective-permute-start | bytes 1179656 | tf_op jit(solution)/shard_map/ppermute | solution.py:40
  163.5 31.4 %collective-permute-start.39 = (bf16[1,1536,384]{2,1,0:T(8,128)(2,1)S(1)}, bf16[1,1536,384]{2,1,0:T(8,128)(2,1)S(1)}, u32[]{:S(2)}, u32[]{:S(2)}) collective-permute-start(bf16[1,1536,384]{2,1,0:T(8,128)(2,1)S(1)} %get-tuple-element.61), channel_id=1, source_target_pairs={{0,1},{1,0},{2,3},{3,2},{4,5},{5,4},{6,7},{7,6},{8,9},{9,8},{10,11... | collective-permute-start | bytes 3538952 | tf_op jit(solution)/shard_map/ppermute | solution.py:40
  166.0 30.1 %collective-permute-start.40 = (bf16[1,384,1536]{2,1,0:T(8,128)(2,1)S(1)}, bf16[1,384,1536]{2,1,0:T(8,128)(2,1)S(1)}, u32[]{:S(2)}, u32[]{:S(2)}) collective-permute-start(bf16[1,384,1536]{2,1,0:T(8,128)(2,1)S(1)} %get-tuple-element.62), channel_id=1, source_target_pairs={{0,1},{1,0},{2,3},{3,2},{4,5},{5,4},{6,7},{7,6},{8,9},{9,8},{10,11... | collective-permute-start | bytes 3538952 | tf_op jit(solution)/shard_map/ppermute | solution.py:40
  166.7 15.0 %collective-permute-start.17 = (bf16[128,1536]{1,0:T(8,128)(2,1)S(1)}, bf16[128,1536]{1,0:T(8,128)(2,1)S(1)}, u32[]{:S(2)}, u32[]{:S(2)}) collective-permute-start(bf16[128,1536]{1,0:T(8,128)(2,1)S(1)} %add_convert_fusion.5), channel_id=1, source_target_pairs={{0,4},{1,5},{2,6},{3,7},{12,8},{13,9},{14,10},{15,11},{16,20},{17,... | collective-permute-start | bytes 1179656 | tf_op jit(solution)/shard_map/ppermute | solution.py:40
  168.1 55.8 %collective-permute-start.37 = (bf16[1,1536,384]{2,1,0:T(8,128)(2,1)S(1)}, bf16[1,1536,384]{2,1,0:T(8,128)(2,1)S(1)}, u32[]{:S(2)}, u32[]{:S(2)}) collective-permute-start(bf16[1,1536,384]{2,1,0:T(8,128)(2,1)S(1)} %get-tuple-element.59), channel_id=1, source_target_pairs={{0,1},{1,0},{2,3},{3,2},{4,5},{5,4},{6,7},{7,6},{8,9},{9,8},{10,11... | collective-permute-start | bytes 3538952 | tf_op jit(solution)/shard_map/ppermute | solution.py:40
  191.7 32.3 %collective-permute-start.38 = (bf16[1,384,1536]{2,1,0:T(8,128)(2,1)S(1)}, bf16[1,384,1536]{2,1,0:T(8,128)(2,1)S(1)}, u32[]{:S(2)}, u32[]{:S(2)}) collective-permute-start(bf16[1,384,1536]{2,1,0:T(8,128)(2,1)S(1)} %get-tuple-element.60), channel_id=1, source_target_pairs={{0,1},{1,0},{2,3},{3,2},{4,5},{5,4},{6,7},{7,6},{8,9},{9,8},{10,11... | collective-permute-start | bytes 3538952 | tf_op jit(solution)/shard_map/ppermute | solution.py:40
  191.8 23.2 %collective-permute-start.15 = (bf16[128,1536]{1,0:T(8,128)(2,1)S(1)}, bf16[128,1536]{1,0:T(8,128)(2,1)S(1)}, u32[]{:S(2)}, u32[]{:S(2)}) collective-permute-start(bf16[128,1536]{1,0:T(8,128)(2,1)S(1)} %add_convert_fusion.5), channel_id=1, source_target_pairs={{4,24},{5,25},{6,26},{7,27},{8,20},{9,21},{10,22},{11,23},{20,8},{... | collective-permute-start | bytes 1179656 | tf_op jit(solution)/shard_map/ppermute | solution.py:40
  194.9 28.1 %collective-permute-start.27 = (bf16[128,1536]{1,0:T(8,128)(2,1)S(1)}, bf16[128,1536]{1,0:T(8,128)(2,1)S(1)}, u32[]{:S(2)}, u32[]{:S(2)}) collective-permute-start(bf16[128,1536]{1,0:T(8,128)(2,1)S(1)} %add_convert_fusion.1), channel_id=1, source_target_pairs={{0,16},{1,17},{2,18},{3,19},{4,20},{5,21},{6,22},{7,23},{8,24},{9,... | collective-permute-start | bytes 1179656 | tf_op jit(solution)/shard_map/ppermute | solution.py:40
  196.2 26.8 %collective-permute-start.18 = (bf16[128,1536]{1,0:T(8,128)(2,1)S(1)}, bf16[128,1536]{1,0:T(8,128)(2,1)S(1)}, u32[]{:S(2)}, u32[]{:S(2)}) collective-permute-start(bf16[128,1536]{1,0:T(8,128)(2,1)S(1)} %add_convert_fusion.3), channel_id=1, source_target_pairs={{0,24},{1,25},{2,26},{3,27},{4,28},{5,29},{6,30},{7,31},{8,16},{9,... | collective-permute-start | bytes 1179656 | tf_op jit(solution)/shard_map/ppermute | solution.py:40
  (15 other events, 251.6 us)

commit v2 on v1

--- a/solution.py
+++ b/solution.py
@@ -87,7 +87,7 @@
     a_refs, c_refs = refs[:n], refs[n:2 * n]
     up_refs, down_refs = refs[2 * n:2 * n + 2], refs[2 * n + 2:2 * n + 4]
     outs = refs[2 * n + 4:]
-    part_refs, grad_rows_ref, cot_ref, slot_ref = outs[:n], outs[n], outs[n + 1], outs[n + 2]
+    part_refs, (grad_rows_ref, cot_ref, act_ref, slot_ref) = outs[:n], outs[n:]
     groups = 2 * local
     slots = groups * cap
     tokens = c_refs[0].shape[0]
@@ -99,6 +99,7 @@
     for g in range(groups):
         grad_hidden = dot(cot_ref[g], down_refs[g // local][g % local], NT)
         act = jnp.concatenate([a_refs[k][g * cap:(g + 1) * cap, :] for k in range(n)], axis=0)
+        act_ref[g] = act
         grad_rows = (grad_hidden * act.astype(F32)).astype(BF16)
         grad_rows_ref[g] = grad_rows
         slot_grad = dot(grad_rows, up_refs[g // local][g % local], NT).astype(BF16)
@@ -117,6 +118,7 @@
     outs = [jax.ShapeDtypeStruct((tokens, width), BF16)] * n + [
         jax.ShapeDtypeStruct((groups, n * cap, hidden), BF16),
         jax.ShapeDtypeStruct((groups, n * cap, width), BF16),
+        jax.ShapeDtypeStruct((groups, n * cap, hidden), BF16),
     ]
     result = pl.pallas_call(
         functools.partial(token_grads_kernel, n, cap, local),
@@ -128,17 +130,18 @@
             flops=4 * groups * n * cap * hidden * width, bytes_accessed=24 << 20, transcendentals=0
         ),
     )(*acts, *cots, *ups, *downs)
-    return result[:n], result[n], result[n + 1]
+    return result[:n], result[n:]
 
 
 def gather_kernel(n, cap, groups, *refs):
-    a_refs, x_refs, out_ref = refs[:n], refs[n:2 * n], refs[2 * n]
+    a_refs, x_refs, out_refs = refs[:n], refs[n:2 * n], refs[2 * n:]
     tokens = x_refs[0].shape[0]
+    local = groups // 2
     for k in range(n):
         pick = selection(a_refs[k], groups * cap, tokens, 0, groups * cap)
         rows = dot(pick, x_refs[k][...], TN).astype(BF16)
         for g in range(groups):
-            out_ref[g, k * cap:(k + 1) * cap, :] = rows[g * cap:(g + 1) * cap]
+            out_refs[g // local][g % local, k * cap:(k + 1) * cap, :] = rows[g * cap:(g + 1) * cap]
 
 
 def gather(acts, xs, cap, groups):
@@ -146,7 +149,7 @@
     width = xs[0].shape[1]
     return pl.pallas_call(
         functools.partial(gather_kernel, n, cap, groups),
-        out_shape=jax.ShapeDtypeStruct((groups, n * cap, width), BF16),
+        out_shape=[jax.ShapeDtypeStruct((groups // 2, n * cap, width), BF16)] * 2,
         name="gather",
         compiler_params=pltpu.CompilerParams(vmem_limit_bytes=20 << 20),
         cost_estimate=pl.CostEstimate(
@@ -155,60 +158,45 @@
     )(*acts, *xs)
 
 
-def weight_grads_kernel(n, cap, first, added, *refs):
-    a_refs, (x_ref, up_ref, grad_rows_ref, cot_ref), more = refs[:n], refs[n:n + 4], refs[n + 4:n + 4 + 2 * added]
+def weight_grads_kernel(sets, *refs):
+    x, act, grad_rows, cot = [
+        jnp.concatenate([refs[4 * i + j][0] for i in range(sets)], axis=0) for j in range(4)
+    ]
+    up_ref, *more = refs[4 * sets:-2]
     grad_up_ref, grad_down_ref = refs[-2:]
-    rows = pl.ds(pl.multiple_of((first + pl.program_id(0)) * cap, cap), cap)
-    act = jnp.concatenate([a_ref[rows, :] for a_ref in a_refs], axis=0)
-    hidden = (dot(x_ref[0], up_ref[0]) * act.astype(F32)).astype(BF16)
-    grad_down = dot(hidden, cot_ref[0], TN)
-    grad_up = dot(x_ref[0], grad_rows_ref[0], TN)
-    for i in range(added):
-        grad_up = grad_up + more[2 * i][0].astype(F32)
-        grad_down = grad_down + more[2 * i + 1][0].astype(F32)
+    hidden = (dot(x, up_ref[0]) * act.astype(F32)).astype(BF16)
+    grad_down = dot(hidden, cot, TN)
+    grad_up = dot(x, grad_rows, TN)
+    for i in range(0, len(more), 2):
+        grad_up = grad_up + more[i][0].astype(F32)
+        grad_down = grad_down + more[i + 1][0].astype(F32)
     grad_down_ref[0] = grad_down.astype(BF16)
     grad_up_ref[0] = grad_up.astype(BF16)
 
 
-def weight_grads(acts, x_rows, up, grad_rows, cot_rows, cap, group, count, more=(), total=None, into=()):
-    n = len(acts)
+def weight_grads(sets, up, more=()):
     local, width, hidden = up.shape
-    at = 0 if total is None else group % local
-    total = count if total is None else total
-
-    def whole(v):
-        return pl.BlockSpec(v.shape, lambda i: (0,) * v.ndim)
+    operands = [pair for one_set in sets for pair in one_set] + [(up, 0)] + [(v, 0) for v in more]
 
     def from_(v, j):
         return pl.BlockSpec((1, *v.shape[1:]), lambda i: (j + i, 0, 0))
 
     outs = [
-        jax.ShapeDtypeStruct((total, width, hidden), BF16),
-        jax.ShapeDtypeStruct((total, hidden, width), BF16),
+        jax.ShapeDtypeStruct((local, width, hidden), BF16),
+        jax.ShapeDtypeStruct((local, hidden, width), BF16),
     ]
-    added = [(v, j) for pair, j in more for v in pair]
-    operands = (*acts, x_rows, up, grad_rows, cot_rows, *[v for v, _ in added], *into)
-    before = len(operands) - len(into)
+    rows = sum(one_set[0][0].shape[1] for one_set in sets)
     return pl.pallas_call(
-        functools.partial(weight_grads_kernel, n, cap, group, len(more)),
-        grid=(count,),
-        in_specs=[
-            *[whole(v) for v in acts],
-            from_(x_rows, group),
-            from_(up, group % local),
-            from_(grad_rows, group),
-            from_(cot_rows, group),
-            *[from_(v, j) for v, j in added],
-            *[pl.BlockSpec(memory_space=pl.ANY) for _ in into],
-        ],
-        out_specs=[from_(v, at) for v in outs],
+        functools.partial(weight_grads_kernel, len(sets)),
+        grid=(local,),
+        in_specs=[from_(v, j) for v, j in operands],
+        out_specs=[from_(v, 0) for v in outs],
         out_shape=outs,
-        input_output_aliases={before + i: i for i in range(len(into))},
-        compiler_params=pltpu.CompilerParams(vmem_limit_bytes=20 << 20),
+        compiler_params=pltpu.CompilerParams(vmem_limit_bytes=28 << 20),
         cost_estimate=pl.CostEstimate(
-            flops=6 * count * n * cap * hidden * width, bytes_accessed=count * (8 << 20), transcendentals=0
-        ),
-    )(*operands)
+            flops=6 * local * rows * hidden * width, bytes_accessed=local * (8 << 20), transcendentals=0
+        ),
+    )(*[v for v, _ in operands])
 
 
 def body(inputs, upstream, gate_saved, expert_ids, route_weights, w_up, w_down):
@@ -283,11 +271,12 @@
     groups = 2 * local
     split = zs // 2 * xs
     halves = (range(split), range(split, grid.chips))
-    parts, grad_rows, cot_rows = [None] * grid.chips, [], []
+    parts, slot_rows = [None] * grid.chips, []
     for members in halves:
-        some, rows, cot = token_grads([acts[k] for k in members], [cots[k] for k in members], ups, downs, cap, local)
-        grad_rows.append(rows)
-        cot_rows.append(cot)
+        some, held = token_grads(
+            [acts[k] for k in members], [cots[k] for k in members], ups, downs, cap, local
+        )
+        slot_rows.append(held)
         for k, part in zip(members, some):
             parts[k] = part
 
@@ -314,21 +303,17 @@
     x_rows = []
     for members in halves:
         x_rows.append(gather([acts[k] for k in members], [tokens_all[k] for k in members], cap, groups))
-    sides = []
-    for h, members in enumerate(halves):
-        sides.append(([acts[k] for k in members], x_rows[h]))
+
+    def rows_of(h, p):
+        grad, cot, act = slot_rows[h]
+        return [(x_rows[h][p], 0), (act, p * local), (grad, p * local), (cot, p * local)]
+
     near_half = []
     for p in range(2):
-        near_half.append(weight_grads(*sides[0], ups[p], grad_rows[0], cot_rows[0], cap, p * local, local))
-    far_half = (*sides[1],)
-    given = []
-    for j in range(local):
-        theirs = weight_grads(*far_half, ups[1], grad_rows[1], cot_rows[1], cap, local + j, 1, [(near_half[1], j)])
-        given.append([grid.move(theirs[0], across), grid.move(theirs[1], across)])
-    ours = ()
-    for j in range(local):
-        more = [(near_half[0], j), (given[j], 0)]
-        ours = weight_grads(*far_half, ups[0], grad_rows[1], cot_rows[1], cap, j, 1, more, local, ours)
+        near_half.append(weight_grads([rows_of(0, p)], ups[p]))
+    given = [grid.move(near_half[1][0], across), grid.move(near_half[1][1], across)]
+    sent = [grid.move(v[j:j + local], across) for v, j in rows_of(1, 1)]
+    ours = weight_grads([rows_of(1, 0), [(v, 0) for v in sent]], ups[0], [*near_half[0], *given])
     grad_up, grad_down = ours
     return (delivered, grad_up[None], grad_down[None])
 

time: 230 us -> 219 us (0.952)
  the two profiles are of different devices: /device:TPU:10 before, /device:TPU:0 now
where the time goes in v2:
time: 219 us; the launch traced here: 218 us
  waiting for transfers between devices  120 us (55%)
  starting transfers between devices  56.9 us (26%)
  Pallas kernels  33.9 us (15%)
  other arithmetic  4.16 us (2%)
  local copies, waits for them, and re-layouts  2.59 us (1%)
    ppermute x43, waiting for transfers between devices, move(): return lax.ppermute(block, ('section', 'ep'), pairs)  120 us
    ppermute x43, starting transfers between devices, move(): return lax.ppermute(block, ('section', 'ep'), pairs)  56.9 us
    pallas_call x2, Pallas kernels, token_grads(): pl.pallas_call(functools.partial(token_grads_kernel, n, cap, local), out_...  15.9 us
    pallas_call x3, Pallas kernels, weight_grads(): pl.pallas_call(functools.partial(weight_grads_kernel, len(sets)), grid=(l...  12.4 us
  transfers between devices with their start and end apart: 43, of which 20 were waited for; matrix products, arithmetic and copies ran while one was open for 1% of the time, Pallas kernels for 12%

profile of v2, /device:TPU:0, one launch (start us, length us, event | category | flops | bytes accessed | tf_op | source)
XLA Modules:
  0.0 218.0 jit_solution(7536665589900428476)
XLA Ops:
  4.0 2.9 %prep.1 = (bf16[200,384]{1,0:T(8,128)(2,1)S(1)}, bf16[200,384]{1,0:T(8,128)(2,1)S(1)}, bf16[200,384]{1,0:T(8,128)(2,1)S(1)}, bf16[200,384]{1,0:T(8,128)(2,1)S(1)...) custom-call(s32[1,1024]{1,0:T(1,128)S(1)} %reshape_squeeze.3.ids_ref, ...), custom_call_target="tpu_custom_call" | custom-call | flops 1610612736 | bytes 1572864 | tf_op jit(solution)/shard_map/prep/pallas_call | solution.py:70
  6.9 4.1 %collective-permute-start = (bf16[200,384]{1,0:T(8,128)(2,1)S(1)}, bf16[200,384]{1,0:T(8,128)(2,1)S(1)}, u32[]{:S(2)}, u32[]{:S(2)}) collective-permute-start(bf16[200,384]{1,0:T(8,128)(2,1)S(1)} %get-tuple-element.35), channel_id=1, source_target_pairs={{0,8},{1,9},{2,10},{3,11},{4,12},{5,13},{6,14},{7,15},{8,0},{9,1},... | collective-permute-start | bytes 460808 | tf_op jit(solution)/shard_map/ppermute | solution.py:40
  14.6 2.5 %collective-permute-start.1 = (bf16[200,384]{1,0:T(8,128)(2,1)S(1)}, bf16[200,384]{1,0:T(8,128)(2,1)S(1)}, u32[]{:S(2)}, u32[]{:S(2)}) collective-permute-start(bf16[200,384]{1,0:T(8,128)(2,1)S(1)} %get-tuple-element.36), channel_id=1, source_target_pairs={{0,10},{1,11},{2,8},{3,9},{4,14},{5,15},{6,12},{7,13},{8,2},{9,3},... | collective-permute-start | bytes 460808 | tf_op jit(solution)/shard_map/ppermute | solution.py:40
  19.2 3.7 %collective-permute-start.3 = (bf16[200,384]{1,0:T(8,128)(2,1)S(1)}, bf16[200,384]{1,0:T(8,128)(2,1)S(1)}, u32[]{:S(2)}, u32[]{:S(2)}) collective-permute-start(bf16[200,384]{1,0:T(8,128)(2,1)S(1)} %get-tuple-element.38), channel_id=1, source_target_pairs={{0,14},{1,15},{2,12},{3,13},{4,10},{5,11},{6,8},{7,9},{8,6},{9,7},... | collective-permute-start | bytes 460808 | tf_op jit(solution)/shard_map/ppermute | solution.py:40
  22.9 19.1 %collective-permute-done.1.refs_1_ = bf16[200,384]{1,0:T(8,128)(2,1)S(1)} collective-permute-done((bf16[200,384]{1,0:T(8,128)(2,1)S(1)}, bf16[200,384]{1,0:T(8,128)(2,1)S(1)}, u32[]{:S(2)}, u32[]{:S(2)}) %collective-permute-start.1) | collective-permute-done | bytes 153632 | tf_op jit(solution)/shard_map/ppermute | solution.py:40
  42.3 2.4 %collective-permute-start.20 = (bf16[200,384]{1,0:T(8,128)(2,1)S(1)}, bf16[200,384]{1,0:T(8,128)(2,1)S(1)}, u32[]{:S(2)}, u32[]{:S(2)}) collective-permute-start(bf16[200,384]{1,0:T(8,128)(2,1)S(1)} %get-tuple-element.45), channel_id=1, source_target_pairs={{0,4},{1,5},{2,6},{3,7},{4,0},{5,1},{6,2},{7,3},{8,12},{9,13},{10,... | collective-permute-start | bytes 460808 | tf_op jit(solution)/shard_map/ppermute | solution.py:40
  44.7 3.5 %collective-permute-start.21 = (bf16[200,384]{1,0:T(8,128)(2,1)S(1)}, bf16[200,384]{1,0:T(8,128)(2,1)S(1)}, u32[]{:S(2)}, u32[]{:S(2)}) collective-permute-start(bf16[200,384]{1,0:T(8,128)(2,1)S(1)} %get-tuple-element.46), channel_id=1, source_target_pairs={{0,6},{1,7},{2,4},{3,5},{4,2},{5,3},{6,0},{7,1},{8,14},{9,15},{10,... | collective-permute-start | bytes 460808 | tf_op jit(solution)/shard_map/ppermute | solution.py:40
  48.7 3.7 %collective-permute-done.21.refs_3_ = bf16[200,384]{1,0:T(8,128)(2,1)S(1)} collective-permute-done((bf16[200,384]{1,0:T(8,128)(2,1)S(1)}, bf16[200,384]{1,0:T(8,128)(2,1)S(1)}, u32[]{:S(2)}, u32[]{:S(2)}) %collective-permute-start.21) | collective-permute-done | bytes 153632 | tf_op jit(solution)/shard_map/ppermute | solution.py:40
  57.3 6.6 %collective-permute-done.4.refs_4_ = bf16[128,1536]{1,0:T(8,128)(2,1)} collective-permute-done((bf16[128,1536]{1,0:T(8,128)(2,1)}, bf16[128,1536]{1,0:T(8,128)(2,1)}, u32[]{:S(2)}, u32[]{:S(2)}) %collective-permute-start.4) | collective-permute-done | bytes 393248 | tf_op jit(solution)/shard_map/ppermute | solution.py:40
  64.5 2.4 %collective-permute-done.31 = bf16[128,1536]{1,0:T(8,128)(2,1)} collective-permute-done((bf16[128,1536]{1,0:T(8,128)(2,1)}, bf16[128,1536]{1,0:T(8,128)(2,1)}, u32[]{:S(2)}, u32[]{:S(2)}) %collective-permute-start.31) | collective-permute-done | bytes 393248 | tf_op jit(solution)/shard_map/ppermute | solution.py:40
  67.0 3.6 %collective-permute-start.5 = (bf16[128,1536]{1,0:T(8,128)(2,1)}, bf16[128,1536]{1,0:T(8,128)(2,1)S(1)}, u32[]{:S(2)}, u32[]{:S(2)}) collective-permute-start(bf16[128,1536]{1,0:T(8,128)(2,1)} %collective-permute-done.4.refs_4_), channel_id=1, source_target_pairs={{0,4},{1,5},{2,6},{3,7},{4,0},{5,1},{6,2},{7,3},{8,12},{9,13},{10,... | collective-permute-start | bytes 1179656 | tf_op jit(solution)/shard_map/ppermute | solution.py:40
  73.6 7.2 %collective-permute-done.5.refs_6_ = bf16[128,1536]{1,0:T(8,128)(2,1)S(1)} collective-permute-done((bf16[128,1536]{1,0:T(8,128)(2,1)}, bf16[128,1536]{1,0:T(8,128)(2,1)S(1)}, u32[]{:S(2)}, u32[]{:S(2)}) %collective-permute-start.5) | collective-permute-done | bytes 393248 | tf_op jit(solution)/shard_map/ppermute | solution.py:40
  82.1 7.1 %collective-permute-done.33 = bf16[128,1536]{1,0:T(8,128)(2,1)S(1)} collective-permute-done((bf16[128,1536]{1,0:T(8,128)(2,1)}, bf16[128,1536]{1,0:T(8,128)(2,1)S(1)}, u32[]{:S(2)}, u32[]{:S(2)}) %collective-permute-start.33) | collective-permute-done | bytes 393248 | tf_op jit(solution)/shard_map/ppermute | solution.py:40
  90.6 4.4 %collective-permute-done.8 = bf16[128,1536]{1,0:T(8,128)(2,1)S(1)} collective-permute-done((bf16[128,1536]{1,0:T(8,128)(2,1)S(1)}, bf16[128,1536]{1,0:T(8,128)(2,1)S(1)}, u32[]{:S(2)}, u32[]{:S(2)}) %collective-permute-start.8) | collective-permute-done | bytes 393248 | tf_op jit(solution)/shard_map/ppermute | solution.py:40
  99.4 7.6 %collective-permute-done.23.refs_7_ = bf16[128,1536]{1,0:T(8,128)(2,1)S(1)} collective-permute-done((bf16[128,1536]{1,0:T(8,128)(2,1)S(1)}, bf16[128,1536]{1,0:T(8,128)(2,1)S(1)}, u32[]{:S(2)}, u32[]{:S(2)}) %collective-permute-start.23) | collective-permute-done | bytes 393248 | tf_op jit(solution)/shard_map/ppermute | solution.py:40
  107.5 4.4 %collective-permute-done.10 = bf16[128,1536]{1,0:T(8,128)(2,1)S(1)} collective-permute-done((bf16[128,1536]{1,0:T(8,128)(2,1)S(1)}, bf16[128,1536]{1,0:T(8,128)(2,1)S(1)}, u32[]{:S(2)}, u32[]{:S(2)}) %collective-permute-start.10) | collective-permute-done | bytes 393248 | tf_op jit(solution)/shard_map/ppermute | solution.py:40
  114.5 8.0 %token_grads.3 = (bf16[128,1536]{1,0:T(8,128)(2,1)S(1)}, bf16[128,1536]{1,0:T(8,128)(2,1)S(1)}, bf16[128,1536]{1,0:T(8,128)(2,1)S(1)}, bf16[128,1536]{1,0:T(8,12...) custom-call(bf16[200,384]{1,0:T(8,128)(2,1)S(1)} %get-tuple-element., ...), custom_call_target="tpu_custom_call" | custom-call | flops 1811939328 | bytes 25165824 | tf_op jit(solution)/shard_map/token_grads/pallas_call | solution.py:123
  124.5 3.4 %collective-permute-done.34.refs_7_ = bf16[128,1536]{1,0:T(8,128)(2,1)S(1)} collective-permute-done((bf16[128,1536]{1,0:T(8,128)(2,1)S(1)}, bf16[128,1536]{1,0:T(8,128)(2,1)S(1)}, u32[]{:S(2)}, u32[]{:S(2)}) %collective-permute-start.34) | collective-permute-done | bytes 393248 | tf_op jit(solution)/shard_map/ppermute | solution.py:40
  128.6 2.5 %collective-permute-start.24 = (bf16[128,1536]{1,0:T(8,128)(2,1)S(1)}, bf16[128,1536]{1,0:T(8,128)(2,1)S(1)}, u32[]{:S(2)}, u32[]{:S(2)}) collective-permute-start(bf16[128,1536]{1,0:T(8,128)(2,1)S(1)} %get-tuple-element.47), channel_id=1, source_target_pairs={{0,20},{1,21},{2,22},{3,23},{4,16},{5,17},{6,18},{7,19},{8,28},{9,... | collective-permute-start | bytes 1179656 | tf_op jit(solution)/shard_map/ppermute | solution.py:40
  131.1 5.2 %collective-permute-done.9.refs_5_ = bf16[128,1536]{1,0:T(8,128)(2,1)S(1)} collective-permute-done((bf16[128,1536]{1,0:T(8,128)(2,1)S(1)}, bf16[128,1536]{1,0:T(8,128)(2,1)S(1)}, u32[]{:S(2)}, u32[]{:S(2)}) %collective-permute-start.9) | collective-permute-done | bytes 393248 | tf_op jit(solution)/shard_map/ppermute | solution.py:40
  136.2 4.3 %collective-permute-done.11.refs_7_ = bf16[128,1536]{1,0:T(8,128)(2,1)S(1)} collective-permute-done((bf16[128,1536]{1,0:T(8,128)(2,1)S(1)}, bf16[128,1536]{1,0:T(8,128)(2,1)S(1)}, u32[]{:S(2)}, u32[]{:S(2)}) %collective-permute-start.11) | collective-permute-done | bytes 393248 | tf_op jit(solution)/shard_map/ppermute | solution.py:40
  140.5 7.9 %token_grads.2 = (bf16[128,1536]{1,0:T(8,128)(2,1)S(1)}, bf16[128,1536]{1,0:T(8,128)(2,1)S(1)}, bf16[128,1536]{1,0:T(8,128)(2,1)S(1)}, bf16[128,1536]{1,0:T(8,12...) custom-call(bf16[200,384]{1,0:T(8,128)(2,1)S(1)} %collective-permute, ...), custom_call_target="tpu_custom_call" | custom-call | flops 1811939328 | bytes 25165824 | tf_op jit(solution)/shard_map/token_grads/pallas_call | solution.py:123
  149.2 4.1 %shard_map.95 = (bf16[2,1536,384]{2,1,0:T(8,128)(2,1)S(1)}, bf16[2,384,1536]{2,1,0:T(8,128)(2,1)S(1)}) custom-call(bf16[2,192,1536]{2,1,0:T(8,128)(2,1)S(1)} %get-tuple-element.62.refs_0_, bf16[4,192,384]{2,1,0:T(8,128)(2,1)S(1)} %get-tuple-element.57.refs_1_, bf16[4,192,384]{2,1,0:T(8,128)(2,1)S(1)} %get-tuple-element.58.refs_2_, ...), custom_call_target="tpu_custom_call" | custom-call | flops 1358954496 | bytes 16777216 | tf_op jit(solution)/shard_map/pallas_call | solution.py:189
  153.9 6.1 %collective-permute-done.14 = bf16[128,1536]{1,0:T(8,128)(2,1)S(1)} collective-permute-done((bf16[128,1536]{1,0:T(8,128)(2,1)S(1)}, bf16[128,1536]{1,0:T(8,128)(2,1)S(1)}, u32[]{:S(2)}, u32[]{:S(2)}) %collective-permute-start.14) | collective-permute-done | bytes 393248 | tf_op jit(solution)/shard_map/ppermute | solution.py:40
  162.3 4.0 %collective-permute-start.17 = (bf16[128,1536]{1,0:T(8,128)(2,1)S(1)}, bf16[128,1536]{1,0:T(8,128)(2,1)S(1)}, u32[]{:S(2)}, u32[]{:S(2)}) collective-permute-start(bf16[128,1536]{1,0:T(8,128)(2,1)S(1)} %add_convert_fusion.5), channel_id=1, source_target_pairs={{0,4},{1,5},{2,6},{3,7},{12,8},{13,9},{14,10},{15,11},{16,20},{17,... | collective-permute-start | bytes 1179656 | tf_op jit(solution)/shard_map/ppermute | solution.py:40
  166.3 5.7 %collective-permute-done.26 = bf16[128,1536]{1,0:T(8,128)(2,1)S(1)} collective-permute-done((bf16[128,1536]{1,0:T(8,128)(2,1)S(1)}, bf16[128,1536]{1,0:T(8,128)(2,1)S(1)}, u32[]{:S(2)}, u32[]{:S(2)}) %collective-permute-start.26) | collective-permute-done | bytes 393248 | tf_op jit(solution)/shard_map/ppermute | solution.py:40
  173.0 6.0 %collective-permute-done.16 = bf16[128,1536]{1,0:T(8,128)(2,1)S(1)} collective-permute-done((bf16[128,1536]{1,0:T(8,128)(2,1)S(1)}, bf16[128,1536]{1,0:T(8,128)(2,1)S(1)}, u32[]{:S(2)}, u32[]{:S(2)}) %collective-permute-start.16) | collective-permute-done | bytes 393248 | tf_op jit(solution)/shard_map/ppermute | solution.py:40
  181.3 9.4 %collective-permute-done.27 = bf16[128,1536]{1,0:T(8,128)(2,1)S(1)} collective-permute-done((bf16[128,1536]{1,0:T(8,128)(2,1)S(1)}, bf16[128,1536]{1,0:T(8,128)(2,1)S(1)}, u32[]{:S(2)}, u32[]{:S(2)}) %collective-permute-start.27) | collective-permute-done | bytes 393248 | tf_op jit(solution)/shard_map/ppermute | solution.py:40
  190.7 4.7 %collective-permute-start.18 = (bf16[128,1536]{1,0:T(8,128)(2,1)S(1)}, bf16[128,1536]{1,0:T(8,128)(2,1)S(1)}, u32[]{:S(2)}, u32[]{:S(2)}) collective-permute-start(bf16[128,1536]{1,0:T(8,128)(2,1)S(1)} %add_convert_fusion.3), channel_id=1, source_target_pairs={{0,24},{1,25},{2,26},{3,27},{4,28},{5,29},{6,30},{7,31},{8,16},{9,... | collective-permute-start | bytes 1179656 | tf_op jit(solution)/shard_map/ppermute | solution.py:40
  195.4 2.8 %shard_map.94 = (bf16[2,1536,384]{2,1,0:T(8,128)(2,1)S(1)}, bf16[2,384,1536]{2,1,0:T(8,128)(2,1)S(1)}) custom-call(bf16[2,192,1536]{2,1,0:T(8,128)(2,1)S(1)} %get-tuple-element.56.refs_0_, bf16[4,192,384]{2,1,0:T(8,128)(2,1)S(1)} %get-tuple-element.57.refs_1_, bf16[4,192,384]{2,1,0:T(8,128)(2,1)S(1)} %get-tuple-element.58.refs_2_, ...), custom_call_target="tpu_custom_call" | custom-call | flops 1358954496 | bytes 16777216 | tf_op jit(solution)/shard_map/pallas_call | solution.py:189
  198.2 12.7 %collective-permute-done.18 = bf16[128,1536]{1,0:T(8,128)(2,1)S(1)} collective-permute-done((bf16[128,1536]{1,0:T(8,128)(2,1)S(1)}, bf16[128,1536]{1,0:T(8,128)(2,1)S(1)}, u32[]{:S(2)}, u32[]{:S(2)}) %collective-permute-start.18) | collective-permute-done | bytes 393248 | tf_op jit(solution)/shard_map/ppermute | solution.py:40
  212.5 5.5 %shard_map.96 = (bf16[2,1536,384]{2,1,0:T(8,128)(2,1)}, bf16[2,384,1536]{2,1,0:T(8,128)(2,1)}) custom-call(bf16[2,192,1536]{2,1,0:T(8,128)(2,1)S(1)} %get-tuple-element.51.refs_0_, bf16[4,192,384]{2,1,0:T(8,128)(2,1)S(1)} %get-tuple-element.52.refs_1_, bf16[4,192,384]{2,1,0:T(8,128)(2,1)S(1)} %get-tuple-element.53.refs_2_, ...), custom_call_target="tpu_custom_call" | custom-call | flops 2717908992 | bytes 16777216 | tf_op jit(solution)/shard_map/pallas_call | solution.py:189
  (89 shorter events, 39.5 us)
Async XLA Ops:
  6.9 12.3 %collective-permute-start = (bf16[200,384]{1,0:T(8,128)(2,1)S(1)}, bf16[200,384]{1,0:T(8,128)(2,1)S(1)}, u32[]{:S(2)}, u32[]{:S(2)}) collective-permute-start(bf16[200,384]{1,0:T(8,128)(2,1)S(1)} %get-tuple-element.35), channel_id=1, source_target_pairs={{0,8},{1,9},{2,10},{3,11},{4,12},{5,13},{6,14},{7,15},{8,0},{9,1},... | collective-permute-start | bytes 460808 | tf_op jit(solution)/shard_map/ppermute | solution.py:40
  11.0 43.5 %collective-permute-start.30 = (bf16[128,1536]{1,0:T(8,128)(2,1)S(1)}, bf16[128,1536]{1,0:T(8,128)(2,1)}, u32[]{:S(2)}, u32[]{:S(2)}) collective-permute-start(bf16[128,1536]{1,0:T(8,128)(2,1)S(1)} %bitcast.16), channel_id=1, source_target_pairs={{4,8},{5,9},{6,10},{7,11},{8,4},{9,5},{10,6},{11,7},{20,24},{21,25... | collective-permute-start | bytes 1179656 | tf_op jit(solution)/shard_map/ppermute | solution.py:40
  12.5 43.4 %collective-permute-start.28 = (bf16[128,1536]{1,0:T(8,128)(2,1)S(1)}, bf16[128,1536]{1,0:T(8,128)(2,1)}, u32[]{:S(2)}, u32[]{:S(2)}) collective-permute-start(bf16[128,1536]{1,0:T(8,128)(2,1)S(1)} %bitcast.17), channel_id=1, source_target_pairs={{0,4},{1,5},{2,6},{3,7},{4,0},{5,1},{6,2},{7,3},{8,12},{9,13},{10,... | collective-permute-start | bytes 1179656 | tf_op jit(solution)/shard_map/ppermute | solution.py:40
  14.6 27.4 %collective-permute-start.1 = (bf16[200,384]{1,0:T(8,128)(2,1)S(1)}, bf16[200,384]{1,0:T(8,128)(2,1)S(1)}, u32[]{:S(2)}, u32[]{:S(2)}) collective-permute-start(bf16[200,384]{1,0:T(8,128)(2,1)S(1)} %get-tuple-element.36), channel_id=1, source_target_pairs={{0,10},{1,11},{2,8},{3,9},{4,14},{5,15},{6,12},{7,13},{8,2},{9,3},... | collective-permute-start | bytes 460808 | tf_op jit(solution)/shard_map/ppermute | solution.py:40
  17.1 25.2 %collective-permute-start.2 = (bf16[200,384]{1,0:T(8,128)(2,1)S(1)}, bf16[200,384]{1,0:T(8,128)(2,1)S(1)}, u32[]{:S(2)}, u32[]{:S(2)}) collective-permute-start(bf16[200,384]{1,0:T(8,128)(2,1)S(1)} %get-tuple-element.37), channel_id=1, source_target_pairs={{0,12},{1,13},{2,14},{3,15},{4,8},{5,9},{6,10},{7,11},{8,4},{9,5},... | collective-permute-start | bytes 460808 | tf_op jit(solution)/shard_map/ppermute | solution.py:40
  19.2 25.5 %collective-permute-start.3 = (bf16[200,384]{1,0:T(8,128)(2,1)S(1)}, bf16[200,384]{1,0:T(8,128)(2,1)S(1)}, u32[]{:S(2)}, u32[]{:S(2)}) collective-permute-start(bf16[200,384]{1,0:T(8,128)(2,1)S(1)} %get-tuple-element.38), channel_id=1, source_target_pairs={{0,14},{1,15},{2,12},{3,13},{4,10},{5,11},{6,8},{7,9},{8,6},{9,7},... | collective-permute-start | bytes 460808 | tf_op jit(solution)/shard_map/ppermute | solution.py:40
  48.2 64.2 %collective-permute-start.12 = (bf16[2,1536,384]{2,1,0:T(8,128)(2,1)S(1)}, bf16[2,1536,384]{2,1,0:T(8,128)(2,1)}, u32[]{:S(2)}, u32[]{:S(2)}) collective-permute-start(bf16[2,1536,384]{2,1,0:T(8,128)(2,1)S(1)} %bitcast.11), channel_id=1, source_target_pairs={{0,1},{1,0},{2,3},{3,2},{4,5},{5,4},{6,7},{7,6},{8,9},{9,8},{10,11... | collective-permute-start | bytes 7077896 | tf_op jit(solution)/shard_map/ppermute | solution.py:40
  48.2 65.8 %collective-permute-start.13 = (bf16[2,384,1536]{2,1,0:T(8,128)(2,1)}, bf16[2,384,1536]{2,1,0:T(8,128)(2,1)}, u32[]{:S(2)}, u32[]{:S(2)}) collective-permute-start(bf16[2,384,1536]{2,1,0:T(8,128)(2,1)} %bitcast.4.refs_10_), channel_id=1, source_target_pairs={{0,1},{1,0},{2,3},{3,2},{4,5},{5,4},{6,7},{7,6},{8,9},{9,8},{10,11... | collective-permute-start | bytes 7077896 | tf_op jit(solution)/shard_map/ppermute | solution.py:40
  54.6 12.4 %collective-permute-start.31 = (bf16[128,1536]{1,0:T(8,128)(2,1)}, bf16[128,1536]{1,0:T(8,128)(2,1)}, u32[]{:S(2)}, u32[]{:S(2)}) collective-permute-start(bf16[128,1536]{1,0:T(8,128)(2,1)} %collective-permute-done.30), channel_id=1, source_target_pairs={{4,0},{5,1},{6,2},{7,3},{8,12},{9,13},{10,14},{11,15},{20,16},{21,... | collective-permute-start | bytes 1179656 | tf_op jit(solution)/shard_map/ppermute | solution.py:40
  55.9 14.8 %collective-permute-start.29 = (bf16[128,1536]{1,0:T(8,128)(2,1)}, bf16[128,1536]{1,0:T(8,128)(2,1)}, u32[]{:S(2)}, u32[]{:S(2)}) collective-permute-start(bf16[128,1536]{1,0:T(8,128)(2,1)} %collective-permute-done.28.refs_6_), channel_id=1, source_target_pairs={{4,8},{5,9},{6,10},{7,11},{8,4},{9,5},{10,6},{11,7},{20,24},{21,25... | collective-permute-start | bytes 1179656 | tf_op jit(solution)/shard_map/ppermute | solution.py:40
  67.0 13.8 %collective-permute-start.5 = (bf16[128,1536]{1,0:T(8,128)(2,1)}, bf16[128,1536]{1,0:T(8,128)(2,1)S(1)}, u32[]{:S(2)}, u32[]{:S(2)}) collective-permute-start(bf16[128,1536]{1,0:T(8,128)(2,1)} %collective-permute-done.4.refs_4_), channel_id=1, source_target_pairs={{0,4},{1,5},{2,6},{3,7},{4,0},{5,1},{6,2},{7,3},{8,12},{9,13},{10,... | collective-permute-start | bytes 1179656 | tf_op jit(solution)/shard_map/ppermute | solution.py:40
  70.6 18.6 %collective-permute-start.33 = (bf16[128,1536]{1,0:T(8,128)(2,1)}, bf16[128,1536]{1,0:T(8,128)(2,1)S(1)}, u32[]{:S(2)}, u32[]{:S(2)}) collective-permute-start(bf16[128,1536]{1,0:T(8,128)(2,1)} %collective-permute-done.29), channel_id=1, source_target_pairs={{4,0},{5,1},{6,2},{7,3},{8,12},{9,13},{10,14},{11,15},{20,16},{21,... | collective-permute-start | bytes 1179656 | tf_op jit(solution)/shard_map/ppermute | solution.py:40
  73.0 17.0 %collective-permute-start.22 = (bf16[128,1536]{1,0:T(8,128)(2,1)}, bf16[128,1536]{1,0:T(8,128)(2,1)S(1)}, u32[]{:S(2)}, u32[]{:S(2)}) collective-permute-start(bf16[128,1536]{1,0:T(8,128)(2,1)} %collective-permute-done.4.refs_4_), channel_id=1, source_target_pairs={{0,2},{1,3},{2,0},{3,1},{4,6},{5,7},{6,4},{7,5},{8,10},{9,11},{10,... | collective-permute-start | bytes 1179656 | tf_op jit(solution)/shard_map/ppermute | solution.py:40
  80.8 14.2 %collective-permute-start.8 = (bf16[128,1536]{1,0:T(8,128)(2,1)S(1)}, bf16[128,1536]{1,0:T(8,128)(2,1)S(1)}, u32[]{:S(2)}, u32[]{:S(2)}) collective-permute-start(bf16[128,1536]{1,0:T(8,128)(2,1)S(1)} %collective-permute-done.7), channel_id=1, source_target_pairs={{4,0},{5,1},{6,2},{7,3},{8,12},{9,13},{10,14},{11,15},{20,16},{21,... | collective-permute-start | bytes 1179656 | tf_op jit(solution)/shard_map/ppermute | solution.py:40
  95.0 12.0 %collective-permute-start.23 = (bf16[128,1536]{1,0:T(8,128)(2,1)S(1)}, bf16[128,1536]{1,0:T(8,128)(2,1)S(1)}, u32[]{:S(2)}, u32[]{:S(2)}) collective-permute-start(bf16[128,1536]{1,0:T(8,128)(2,1)S(1)} %collective-permute-done.22.refs_5_), channel_id=1, source_target_pairs={{0,4},{1,5},{2,6},{3,7},{4,0},{5,1},{6,2},{7,3},{8,12},{9,13},{10,... | collective-permute-start | bytes 1179656 | tf_op jit(solution)/shard_map/ppermute | solution.py:40
  95.0 16.9 %collective-permute-start.10 = (bf16[128,1536]{1,0:T(8,128)(2,1)S(1)}, bf16[128,1536]{1,0:T(8,128)(2,1)S(1)}, u32[]{:S(2)}, u32[]{:S(2)}) collective-permute-start(bf16[128,1536]{1,0:T(8,128)(2,1)S(1)} %collective-permute-done.6), channel_id=1, source_target_pairs={{4,0},{5,1},{6,2},{7,3},{8,12},{9,13},{10,14},{11,15},{20,16},{21,... | collective-permute-start | bytes 1179656 | tf_op jit(solution)/shard_map/ppermute | solution.py:40
  98.8 23.8 %collective-permute-start.40 = (bf16[128,1536]{1,0:T(8,128)(2,1)}, bf16[128,1536]{1,0:T(8,128)(2,1)S(1)}, u32[]{:S(2)}, u32[]{:S(2)}) collective-permute-start(bf16[128,1536]{1,0:T(8,128)(2,1)} %collective-permute-done.28.refs_6_), channel_id=1, source_target_pairs={{0,2},{1,3},{2,0},{3,1},{4,6},{5,7},{6,4},{7,5},{8,10},{9,11},{10,... | collective-permute-start | bytes 1179656 | tf_op jit(solution)/shard_map/ppermute | solution.py:40
  107.0 17.5 %collective-permute-start.32 = (bf16[128,1536]{1,0:T(8,128)(2,1)S(1)}, bf16[128,1536]{1,0:T(8,128)(2,1)S(1)}, u32[]{:S(2)}, u32[]{:S(2)}) collective-permute-start(bf16[128,1536]{1,0:T(8,128)(2,1)S(1)} %broadcast_select_fusion.1.refs_4_), channel_id=1, source_target_pairs={{0,2},{1,3},{2,0},{3,1},{4,6},{5,7},{6,4},{7,5},{8,10},{9,11},{10,... | collective-permute-start | bytes 1179656 | tf_op jit(solution)/shard_map/ppermute | solution.py:40
  111.9 15.9 %collective-permute-start.34 = (bf16[128,1536]{1,0:T(8,128)(2,1)S(1)}, bf16[128,1536]{1,0:T(8,128)(2,1)S(1)}, u32[]{:S(2)}, u32[]{:S(2)}) collective-permute-start(bf16[128,1536]{1,0:T(8,128)(2,1)S(1)} %broadcast_select_fusion.refs_6_), channel_id=1, source_target_pairs={{0,2},{1,3},{2,0},{3,1},{4,6},{5,7},{6,4},{7,5},{8,10},{9,11},{10,... | collective-permute-start | bytes 1179656 | tf_op jit(solution)/shard_map/ppermute | solution.py:40
  112.4 23.8 %collective-permute-start.9 = (bf16[128,1536]{1,0:T(8,128)(2,1)S(1)}, bf16[128,1536]{1,0:T(8,128)(2,1)S(1)}, u32[]{:S(2)}, u32[]{:S(2)}) collective-permute-start(bf16[128,1536]{1,0:T(8,128)(2,1)S(1)} %broadcast_select_fusion.3.refs_4_), channel_id=1, source_target_pairs={{0,2},{1,3},{2,0},{3,1},{4,6},{5,7},{6,4},{7,5},{8,10},{9,11},{10,... | collective-permute-start | bytes 1179656 | tf_op jit(solution)/shard_map/ppermute | solution.py:40
  114.0 26.5 %collective-permute-start.11 = (bf16[128,1536]{1,0:T(8,128)(2,1)S(1)}, bf16[128,1536]{1,0:T(8,128)(2,1)S(1)}, u32[]{:S(2)}, u32[]{:S(2)}) collective-permute-start(bf16[128,1536]{1,0:T(8,128)(2,1)S(1)} %broadcast_select_fusion.2.refs_6_), channel_id=1, source_target_pairs={{0,2},{1,3},{2,0},{3,1},{4,6},{5,7},{6,4},{7,5},{8,10},{9,11},{10,... | collective-permute-start | bytes 1179656 | tf_op jit(solution)/shard_map/ppermute | solution.py:40
  122.6 30.9 %collective-permute-start.25 = (bf16[128,1536]{1,0:T(8,128)(2,1)S(1)}, bf16[128,1536]{1,0:T(8,128)(2,1)S(1)}, u32[]{:S(2)}, u32[]{:S(2)}) collective-permute-start(bf16[128,1536]{1,0:T(8,128)(2,1)S(1)} %get-tuple-element.50), channel_id=1, source_target_pairs={{0,4},{1,5},{2,6},{3,7},{4,0},{5,1},{6,2},{7,3},{8,12},{9,13},{10,... | collective-permute-start | bytes 1179656 | tf_op jit(solution)/shard_map/ppermute | solution.py:40
  128.6 33.6 %collective-permute-start.24 = (bf16[128,1536]{1,0:T(8,128)(2,1)S(1)}, bf16[128,1536]{1,0:T(8,128)(2,1)S(1)}, u32[]{:S(2)}, u32[]{:S(2)}) collective-permute-start(bf16[128,1536]{1,0:T(8,128)(2,1)S(1)} %get-tuple-element.47), channel_id=1, source_target_pairs={{0,20},{1,21},{2,22},{3,23},{4,16},{5,17},{6,18},{7,19},{8,28},{9,... | collective-permute-start | bytes 1179656 | tf_op jit(solution)/shard_map/ppermute | solution.py:40
  148.5 12.2 %collective-permute-start.37 = (bf16[2,192,384]{2,1,0:T(8,128)(2,1)S(1)}, bf16[2,192,384]{2,1,0:T(8,128)(2,1)S(1)}, u32[]{:S(2)}, u32[]{:S(2)}) collective-permute-start(bf16[2,192,384]{2,1,0:T(8,128)(2,1)S(1)} %slice.10), channel_id=1, source_target_pairs={{0,1},{1,0},{2,3},{3,2},{4,5},{5,4},{6,7},{7,6},{8,9},{9,8},{10,11... | collective-permute-start | bytes 884744 | tf_op jit(solution)/shard_map/ppermute | solution.py:40
  153.3 59.2 %collective-permute-start.41 = (bf16[2,1536,384]{2,1,0:T(8,128)(2,1)S(1)}, bf16[2,1536,384]{2,1,0:T(8,128)(2,1)S(1)}, u32[]{:S(2)}, u32[]{:S(2)}) collective-permute-start(bf16[2,1536,384]{2,1,0:T(8,128)(2,1)S(1)} %get-tuple-element.63), channel_id=1, source_target_pairs={{0,1},{1,0},{2,3},{3,2},{4,5},{5,4},{6,7},{7,6},{8,9},{9,8},{10,11... | collective-permute-start | bytes 7077896 | tf_op jit(solution)/shard_map/ppermute | solution.py:40
  153.5 59.0 %collective-permute-start.42 = (bf16[2,384,1536]{2,1,0:T(8,128)(2,1)S(1)}, bf16[2,384,1536]{2,1,0:T(8,128)(2,1)S(1)}, u32[]{:S(2)}, u32[]{:S(2)}) collective-permute-start(bf16[2,384,1536]{2,1,0:T(8,128)(2,1)S(1)} %get-tuple-element.64), channel_id=1, source_target_pairs={{0,1},{1,0},{2,3},{3,2},{4,5},{5,4},{6,7},{7,6},{8,9},{9,8},{10,11... | collective-permute-start | bytes 7077896 | tf_op jit(solution)/shard_map/ppermute | solution.py:40
  160.1 12.0 %collective-permute-start.26 = (bf16[128,1536]{1,0:T(8,128)(2,1)S(1)}, bf16[128,1536]{1,0:T(8,128)(2,1)S(1)}, u32[]{:S(2)}, u32[]{:S(2)}) collective-permute-start(bf16[128,1536]{1,0:T(8,128)(2,1)S(1)} %add_convert_fusion.2), channel_id=1, source_target_pairs={{0,2},{1,3},{2,0},{3,1},{4,6},{5,7},{6,4},{7,5},{8,10},{9,11},{10,... | collective-permute-start | bytes 1179656 | tf_op jit(solution)/shard_map/ppermute | solution.py:40
  160.7 18.4 %collective-permute-start.16 = (bf16[128,1536]{1,0:T(8,128)(2,1)S(1)}, bf16[128,1536]{1,0:T(8,128)(2,1)S(1)}, u32[]{:S(2)}, u32[]{:S(2)}) collective-permute-start(bf16[128,1536]{1,0:T(8,128)(2,1)S(1)} %get-tuple-element.42), channel_id=1, source_target_pairs={{0,2},{1,3},{2,0},{3,1},{4,6},{5,7},{6,4},{7,5},{8,10},{9,11},{10,... | collective-permute-start | bytes 1179656 | tf_op jit(solution)/shard_map/ppermute | solution.py:40
  162.3 16.8 %collective-permute-start.17 = (bf16[128,1536]{1,0:T(8,128)(2,1)S(1)}, bf16[128,1536]{1,0:T(8,128)(2,1)S(1)}, u32[]{:S(2)}, u32[]{:S(2)}) collective-permute-start(bf16[128,1536]{1,0:T(8,128)(2,1)S(1)} %add_convert_fusion.5), channel_id=1, source_target_pairs={{0,4},{1,5},{2,6},{3,7},{12,8},{13,9},{14,10},{15,11},{16,20},{17,... | collective-permute-start | bytes 1179656 | tf_op jit(solution)/shard_map/ppermute | solution.py:40
  179.1 33.4 %collective-permute-start.35 = (bf16[2,192,1536]{2,1,0:T(8,128)(2,1)S(1)}, bf16[2,192,1536]{2,1,0:T(8,128)(2,1)S(1)}, u32[]{:S(2)}, u32[]{:S(2)}) collective-permute-start(bf16[2,192,1536]{2,1,0:T(8,128)(2,1)S(1)} %get-tuple-element.55), channel_id=1, source_target_pairs={{0,1},{1,0},{2,3},{3,2},{4,5},{5,4},{6,7},{7,6},{8,9},{9,8},{10,11... | collective-permute-start | bytes 3538952 | tf_op jit(solution)/shard_map/ppermute | solution.py:40
  179.1 33.4 %collective-permute-start.38 = (bf16[2,192,1536]{2,1,0:T(8,128)(2,1)S(1)}, bf16[2,192,1536]{2,1,0:T(8,128)(2,1)S(1)}, u32[]{:S(2)}, u32[]{:S(2)}) collective-permute-start(bf16[2,192,1536]{2,1,0:T(8,128)(2,1)S(1)} %slice.11), channel_id=1, source_target_pairs={{0,1},{1,0},{2,3},{3,2},{4,5},{5,4},{6,7},{7,6},{8,9},{9,8},{10,11... | collective-permute-start | bytes 3538952 | tf_op jit(solution)/shard_map/ppermute | solution.py:40
  190.7 20.2 %collective-permute-start.18 = (bf16[128,1536]{1,0:T(8,128)(2,1)S(1)}, bf16[128,1536]{1,0:T(8,128)(2,1)S(1)}, u32[]{:S(2)}, u32[]{:S(2)}) collective-permute-start(bf16[128,1536]{1,0:T(8,128)(2,1)S(1)} %add_convert_fusion.3), channel_id=1, source_target_pairs={{0,24},{1,25},{2,26},{3,27},{4,28},{5,29},{6,30},{7,31},{8,16},{9,... | collective-permute-start | bytes 1179656 | tf_op jit(solution)/shard_map/ppermute | solution.py:40
  (16 other events, 212.2 us)
